TPU v7x, 32 devices: a whole 2x2x4 slice. The times are simulated.
32 devices in a mesh: row: 4 (over x, core), col: 8 (over z, y).
Axes of the slice: x: 2, y: 2, z: 4, core: 2. Of those that a mesh axis runs over, the one named last changes fastest.
Arguments:
- factor: float32 [1, 8192, 512], P(None, ('row', 'col')), may hold values from -40 to 40, as said below
- update: float32 [1, 8192, 256], P(None, ('row', 'col')), may hold values from -1.5 to 1.5
Outputs:
- new_factor: float32 [1, 8192, 512], P(None, ('row', 'col'))
- new_update: float32 [1, 8192, 256], P(None, ('row', 'col'))
- column_scale: float32 [512], replicated
Inputs may be any that keep to these rules, and one draw needn't show every extreme that they name: `factor`: in the columns of panel p, rows of global tiles before p are zero; the diagonal block of panel p is lower triangular with diagonal entries of 1 to 2.
All inputs are finite; a program needn't handle non-finite values.
Results may differ from a plain program's by a relative error of at most 0.0003.
Values sent between devices are 32-bit elements; how exact they have to be, the bound alone decides.
No kernel may reach another device: no remote copies, remote signals or barrier semaphores. Data moves between devices by JAX's collectives and lax.ppermute only.
A program may use at most 64 MiB of HBM per device.

v0:
```python
import jax
import jax.numpy as jnp
from jax import lax
from jax.sharding import PartitionSpec as P

PW = 256
K = 256
PANELS = 2


def broadcast(array, axis, root):
    mine = lax.axis_index(axis) == root
    return lax.psum(jnp.where(mine, array, jnp.zeros_like(array)), axis)


def panel_terms(block_factor, block_update):
    highest = lax.Precision.HIGHEST
    gram_matrix = jnp.dot(block_factor, block_factor.T, precision=highest) + jnp.dot(
        block_update, block_update.T, precision=highest
    )
    diag_new = jnp.linalg.cholesky(gram_matrix)
    solved = lax.linalg.triangular_solve(block_factor, block_update, left_side=True, lower=True)
    inner_matrix = jnp.eye(K, dtype=jnp.float32) + jnp.dot(solved.T, solved, precision=highest)
    chol_inner = jnp.linalg.cholesky(inner_matrix)
    left_first = lax.linalg.triangular_solve(diag_new, block_factor, left_side=True, lower=True).T
    left_second = lax.linalg.triangular_solve(diag_new, block_update, left_side=True, lower=True).T
    right_first = lax.linalg.triangular_solve(
        chol_inner, jnp.eye(K, dtype=jnp.float32), left_side=True, lower=True
    ).T
    right_second = jnp.dot(solved, right_first, precision=highest)
    return (left_first, left_second, right_first, right_second)


def empty_terms(block_factor, block_update):
    return (
        jnp.zeros((PW, PW), jnp.float32),
        jnp.zeros((K, PW), jnp.float32),
        jnp.zeros((K, K), jnp.float32),
        jnp.zeros((PW, K), jnp.float32),
    )


def advance(panel_cols, current, transforms):
    highest = lax.Precision.HIGHEST
    left_first, left_second, right_first, right_second = transforms
    tile_count = panel_cols.shape[0]
    flat_cols = panel_cols.reshape(-1, PW)
    flat_update = current.reshape(-1, K)
    updated_cols = jnp.dot(flat_cols, left_first, precision=highest) + jnp.dot(
        flat_update, left_second, precision=highest
    )
    updated_rows = jnp.dot(flat_update, right_first, precision=highest) - jnp.dot(
        flat_cols, right_second, precision=highest
    )
    return (updated_cols.reshape(tile_count, PW, PW), updated_rows.reshape(tile_count, PW, K))


def on_device(factor, update):
    device_count = lax.axis_size(("row", "col"))
    my_index = lax.axis_index(("row", "col"))
    row_total = factor.shape[0] * device_count * PW
    current = update
    columns_out = []
    squares = []
    for panel_num in range(PANELS):
        low = panel_num * PW
        panel_cols = factor[:, :, low : low + PW]
        own_terms = lax.cond(
            my_index == panel_num, panel_terms, empty_terms, panel_cols[0], current[0]
        )
        transforms = jax.tree.map(
            lambda part: broadcast(part, ("row", "col"), panel_num), own_terms
        )
        updated_cols, current = advance(panel_cols, current, transforms)
        columns_out.append(updated_cols)
        local_squares = jnp.sum(updated_cols * updated_cols, axis=(0, 1))
        squares.append(lax.psum(local_squares, ("row", "col")))
    stacked = jnp.concatenate(squares, axis=0)
    column_scale = jnp.sqrt(stacked / row_total + 1e-06)
    return (jnp.concatenate(columns_out, axis=2), current, column_scale)


def solution(mesh):
    return jax.shard_map(
        on_device,
        mesh=mesh,
        in_specs=(P(None, ("row", "col"), None), P(None, ("row", "col"), None)),
        out_specs=(P(None, ("row", "col"), None), P(None, ("row", "col"), None), P()),
        check_vma=False,
    )
```

profile of v0, /device:TPU:0, one launch (start us, length us, event | category | flops | bytes accessed | tf_op | source)
XLA Modules:
  0.0 627.2 jit_solution(11467668654431806017)
XLA Ops:
  8.3 150.0 %conditional.2 = (f32[256,256]{1,0:T(8,128)S(1)}, f32[256,256]{1,0:T(8,128)S(1)}, f32[256,256]{1,0:T(8,128)S(1)}, f32[256,256]{1,0:T(8,128)S(1)}) conditional(s32[]{:T(128)} %convert_element_type.18, () %tuple.26, (f32[256,256]{1,0:T(8,128)S(1)}, f32[256,256]{1,0:T(8,128)S(1)}) %tuple.188), branch_computations={%region_0.0_spmd, %region_1.8_spmd} | conditional | flops 1512079872 | bytes 17961552 | solution.py:68
  8.5 3.8 while.17
  11.0 1.3 bitcast_dynamic-update-slice_fusion.16
  12.3 20.2 %custom-call.24 = f32[2,128,128]{1,2,0:T(8,128)S(1)} custom-call(f32[2,128,128]{2,1,0:T(8,128)S(1)} %get-tuple-element.85), custom_call_target="InvertDiagBlocksLowerTriangular" | custom-call | tf_op jit(solution)/shard_map/cond/branch_1_fun/triangular_solve/custom-call.0 | solution.py:22
  34.2 11.7 %cholesky.248 = f32[128,128]{1,0:T(8,128)S(1)} custom-call(f32[128,128]{1,0:T(8,128)S(1)} %cholesky.346), custom_call_target="Cholesky" | custom-call | tf_op jit(solution)/shard_map/cond/branch_1_fun/jit(cholesky)/cholesky | solution.py:24
  46.0 9.8 %custom-call.25 = f32[1,128,128]{1,2,0:T(8,128)S(1)} custom-call(f32[1,128,128]{2,1,0:T(8,128)S(1)} %get-tuple-element.181), custom_call_target="InvertDiagBlocksLowerTriangular" | custom-call | tf_op jit(solution)/shard_map/cond/branch_1_fun/jit(cholesky)/cholesky | solution.py:24
  56.3 11.7 %cholesky.265 = f32[128,128]{1,0:T(8,128)S(1)} custom-call(f32[128,128]{1,0:T(8,128)S(1)} %convolution_subtract_fusion.4), custom_call_target="Cholesky" | custom-call | tf_op jit(solution)/shard_map/cond/branch_1_fun/jit(cholesky)/cholesky | solution.py:24
  70.0 3.8 while.18
  70.6 1.3 bitcast_dynamic-update-slice_fusion.17
  72.5 1.3 bitcast_dynamic-update-slice_fusion.17
  73.8 19.8 %custom-call.26 = f32[2,128,128]{1,2,0:T(8,128)S(1)} custom-call(f32[2,128,128]{2,1,0:T(8,128)S(1)} %get-tuple-element.86), custom_call_target="InvertDiagBlocksLowerTriangular" | custom-call | tf_op jit(solution)/shard_map/cond/branch_1_fun/triangular_solve/custom-call.0 | solution.py:27
  96.3 11.7 %cholesky.214 = f32[128,128]{1,0:T(8,128)S(1)} custom-call(f32[128,128]{1,0:T(8,128)S(1)} %cholesky.349), custom_call_target="Cholesky" | custom-call | tf_op jit(solution)/shard_map/cond/branch_1_fun/jit(cholesky)/cholesky | solution.py:21
  108.0 9.8 %custom-call.21 = f32[1,128,128]{1,2,0:T(8,128)S(1)} custom-call(f32[1,128,128]{2,1,0:T(8,128)S(1)} %get-tuple-element.177), custom_call_target="InvertDiagBlocksLowerTriangular" | custom-call | tf_op jit(solution)/shard_map/cond/branch_1_fun/jit(cholesky)/cholesky | solution.py:21
  118.4 11.9 %cholesky.231 = f32[128,128]{1,0:T(8,128)S(1)} custom-call(f32[128,128]{1,0:T(8,128)S(1)} %convolution_subtract_fusion.5), custom_call_target="Cholesky" | custom-call | tf_op jit(solution)/shard_map/cond/branch_1_fun/jit(cholesky)/cholesky | solution.py:21
  132.3 4.0 while.16
  132.9 1.4 bitcast_dynamic-update-slice_fusion.15
  134.9 1.4 bitcast_dynamic-update-slice_fusion.15
  136.3 19.7 %custom-call.22 = f32[2,128,128]{1,2,0:T(8,128)S(1)} custom-call(f32[2,128,128]{2,1,0:T(8,128)S(1)} %get-tuple-element.83), custom_call_target="InvertDiagBlocksLowerTriangular" | custom-call | tf_op jit(solution)/shard_map/cond/branch_1_fun/triangular_solve/custom-call.0 | solution.py:25
  160.7 124.5 %all-reduce.9.cloned.1.call-done = (f32[256,256]{1,0:T(8,128)}, f32[256,256]{1,0:T(8,128)}) async-done(((f32[256,256]{1,0:T(8,128)}, f32[256,256]{1,0:T(8,128)}), (f32[256,256]{1,0:T(8,128)}, f32[256,256]{1,0:T(8,128)})) %all-reduce.9.cloned.1.call-update) | async-done | bytes 524304 | tf_op jit(solution)/shard_map/psum | solution.py:13
  285.2 1.6 fusion.65
  287.4 4.9 conditional.3
  294.0 279.2 %all-reduce.7.cloned.1.call-done = (f32[256,256]{1,0:T(8,128)}, f32[256,256]{1,0:T(8,128)}, f32[256,256]{1,0:T(8,128)}, f32[256,256]{1,0:T(8,128)}, f32[256,256]{1,0:T(8,128)}, /*index=5*/f32[256,256]{1,0:T(8,128)}) async-done(((f32[256,256]{1,0:T(8,128)}, f32[256,256]{1,0:T(8,128)}, f32[256,256]{1,0:T(8,128)}, f32[256,256]{1,0:T(8,128)}, f32[256,256]{1,0:T(8,128)}, /*index=5*/f32[256,256]{1,0:T(8,128)}), ...) | async-done | bytes 1572880 | tf_op jit(solution)/shard_map/psum | solution.py:13
  573.3 1.6 convolution_bitcast_fusion.1
  580.5 39.0 %all-reduce.1 = (f32[256]{0:T(256)S(1)}, f32[256]{0:T(256)S(1)}) all-reduce(f32[256]{0:T(256)S(1)} %get-tuple-element.214, f32[256]{0:T(256)S(1)} %get-tuple-element.216), channel_id=1, replica_groups=mesh['row'=4,'col'=8] {'row','col'}, use_global_device_ids=true, to_apply=%region_19.22 | all-reduce | flops 512 | bytes 4096 | tf_op jit(solution)/shard_map/psum | solution.py:77
  (101 shorter events, 26.5 us)
Async XLA Ops:
  7.2 278.0 %all-reduce.9.cloned.1.call-start = ((), (), s32[]{:S(2)}) async-start(), calls=%async_computation.1 | async-start | bytes 1048576 | tf_op jit(solution)/shard_map/psum | solution.py:13
  7.2 1.1 copy-start
  159.8 413.4 %all-reduce.7.cloned.1.call-start = ((), (), s32[]{:S(2)}) async-start(), calls=%async_computation | async-start | bytes 3145728 | tf_op jit(solution)/shard_map/psum | solution.py:13
  160.7 126.1 %copy-start.1 = (f32[1,256,512]{2,1,0:T(8,128)S(1)}, f32[1,256,512]{2,1,0:T(8,128)}, u32[]{:S(2)}) copy-start(f32[1,256,512]{2,1,0:T(8,128)} %param.9) | copy-start | bytes 1572868
  285.2 1.6 copy-start.7
  573.3 1.6 copy-start.5
  574.9 1.0 copy-start.4
  575.8 0.9 copy-start.3
  576.8 0.9 copy-start.2
  578.4 1.0 copy-start.6
Sparse Core Ops, SparseCore 0:
  160.0 125.1 all-reduce.8
  294.2 279.0 all-reduce.6
where the time goes:
time: 630 us; the launch traced here: 627 us
  waiting for transfers between devices  404 us (64%)
  other arithmetic  133 us (21%)
  blocking collectives  39 us (6%)
  local copies, waits for them, and re-layouts  16.1 us (3%)
  between operations  14.4 us (2%)
  matrix products  13.8 us (2%)
  loops' own time  7.45 us (1%)
    psum x2, waiting for transfers between devices, broadcast(): return lax.psum(jnp.where(mine, array, jnp.zeros_like(array)), axis)  404 us
    psum x1, blocking collectives, on_device(): squares.append(lax.psum(local_squares, ('row', 'col')))  39 us
    another operation x6, other arithmetic, panel_terms(): diag_new = jnp.linalg.cholesky(gram_matrix)  34.1 us
    another operation x6, other arithmetic, panel_terms(): chol_inner = jnp.linalg.cholesky(inner_matrix)  33.9 us
    another operation x2, other arithmetic, panel_terms(): lax.linalg.triangular_solve(block_factor, block_update, left_side=True, l...  20.2 us
    another operation x2, other arithmetic, panel_terms(): lax.linalg.triangular_solve(chol_inner, jnp.eye(K, dtype=jnp.float32), le...  19.9 us
    another operation x3, other arithmetic, panel_terms(): lax.linalg.triangular_solve(diag_new, block_factor, left_side=True, lower...  19.7 us
  transfers between devices with their start and end apart: 2, of which 2 were waited for; matrix products, arithmetic and copies ran while one was open for 0% of the time, Pallas kernels for 0%

commit v1 on v0

v1 whole, which is shorter than its diff:
```python
import jax
import jax.numpy as jnp
from jax import lax
from jax.experimental import pallas as pl
from jax.experimental.pallas import tpu as pltpu
from jax.sharding import PartitionSpec as P

T = 8
N = 128
NB = N // T
AXES = ("row", "col")
HI = lax.Precision.HIGHEST
F32 = jnp.float32


def dot(a, b, ca, cb):
    return lax.dot_general(a, b, (((ca,), (cb,)), ((), ())), precision=HI, preferred_element_type=F32)


def mm(a, b):
    return dot(a, b, 1, 0)


def mm_nt(a, b):
    return dot(a, b, 1, 1)


def mm_tn(a, b):
    return dot(a, b, 0, 0)


def lane_bcast(x, lane):
    return jnp.broadcast_to(x[:, lane : lane + 1], (T, N))


def row_bcast(ref, row):
    return jnp.broadcast_to(ref[row : row + 1, :], (T, N))


def tiles_of(ref, start):
    return [ref[start + t * T : start + (t + 1) * T, start : start + N] for t in range(NB)]


def store_rows(out, start, k, rows, lane, sub):
    tile = rows[T - 1]
    for j in range(T - 2, -1, -1):
        tile = jnp.where(sub <= j, rows[j], tile)
    out[start + k : start + k + T, start : start + N] = jnp.where(lane <= sub + k, tile, 0.0)


def eliminate(mat, b, rows, inside):
    k = b * T
    for t in range(b + 1, NB):
        cur = mat[t]
        even = jnp.where(inside, 0.0, cur)
        odd = None
        for j in range(T):
            term = lane_bcast(cur, k + j) * rows[j]
            if j % 2 == 0:
                even = even - term
            else:
                odd = term if odd is None else odd + term
        mat[t] = even - odd


def chol_inverse(mats, outs, start, cols, rows_ref):
    lane = lax.broadcasted_iota(jnp.int32, (T, N), 1)
    sub = lax.broadcasted_iota(jnp.int32, (T, N), 0)
    for b in range(NB):
        k = b * T
        inside = (lane >= k) & (lane < k + T)
        unit = (lane == sub + k).astype(F32)
        for q, mat in enumerate(mats):
            sc = cols.at[q, b % 2]
            sr = rows_ref.at[q, b % 2]
            own = mat[b]
            for j in range(T):
                sc[j * T : (j + 1) * T, :] = lane_bcast(own, k + j)
            sr[...] = jnp.where(inside, unit, own)
            a = {(i, j): row_bcast(sc, j * T + i) for j in range(T) for i in range(j, T)}
            r = [row_bcast(sr, j) for j in range(T)]
            low = {}
            inv = []
            for j in range(T):
                scale = lax.rsqrt(a[j, j])
                inv.append(scale)
                for i in range(j + 1, T):
                    low[i, j] = a[i, j] * scale
                for i in range(j + 1, T):
                    for i2 in range(j + 1, i + 1):
                        a[i, i2] = a[i, i2] - low[i, j] * low[i2, j]
                r[j] = r[j] * scale
                for i in range(j + 1, T):
                    r[i] = r[i] - low[i, j] * r[j]
            store_rows(outs[q], start, k, r, lane, sub)
            if b < NB - 1:
                for j in range(T - 1, -1, -1):
                    r[j] = r[j] * inv[j]
                    for i in range(j):
                        r[i] = r[i] - low[j, i] * r[j]
                eliminate(mat, b, r, inside)


def tri_inverse(mats, outs, start, cols, rows_ref):
    lane = lax.broadcasted_iota(jnp.int32, (T, N), 1)
    sub = lax.broadcasted_iota(jnp.int32, (T, N), 0)
    for b in range(NB):
        k = b * T
        inside = (lane >= k) & (lane < k + T)
        unit = (lane == sub + k).astype(F32)
        for q, mat in enumerate(mats):
            sc = cols.at[q, b % 2]
            sr = rows_ref.at[q, b % 2]
            own = mat[b]
            for j in range(T):
                sc[j * T : (j + 1) * T, :] = lane_bcast(own, k + j)
            sr[...] = jnp.where(inside, unit, jnp.where(lane < k, own, 0.0))
            r = [row_bcast(sr, j) for j in range(T)]
            for j in range(T):
                r[j] = r[j] * (1.0 / row_bcast(sc, j * T + j))
                for i in range(j + 1, T):
                    r[i] = r[i] - row_bcast(sc, j * T + i) * r[j]
            store_rows(outs[q], start[q], k, r, lane, sub)
            eliminate(mat, b, r, inside)


def solve_kernel(mine, factor, update, solved, carried, inverse, cols, rows_ref):
    width = update.shape[1]
    low = pl.multiple_of(mine[0] * width, width)
    block = factor.at[:, pl.ds(low, width)]
    tri_inverse(
        [tiles_of(block, 0), tiles_of(block, N)], [inverse, inverse], [0, N], cols, rows_ref
    )
    upper = inverse[:N, :N]
    lower = inverse[N:, N:]
    corner = block[N:, :N]
    for rhs, out in ((update, solved), (factor.at[:, :width], carried)):
        top = mm(upper, rhs[:N, :])
        out[:N, :] = top
        out[N:, :] = mm(lower, rhs[N:, :] - mm(corner, top))


def both_inverses(grams, inverses, cols, rows_ref):
    chol_inverse([tiles_of(g, 0) for g in grams], inverses, 0, cols, rows_ref)
    corners = []
    for gram, inv in zip(grams, inverses):
        corner = mm_nt(gram[N:, :N], inv[:N, :N])
        gram[N:, N:] = gram[N:, N:] - mm_nt(corner, corner)
        corners.append(mm(corner, inv[:N, :N]))
    chol_inverse([tiles_of(g, N) for g in grams], inverses, N, cols, rows_ref)
    for inv, corner in zip(inverses, corners):
        inv[N:, :N] = -mm(inv[N:, N:], corner)
        inv[:N, N:] = jnp.zeros((N, N), F32)


def update_kernel(
    factor, update, first, second, carried, new_factor, new_update, sums,
    gram_l, gram_c, inv_l, inv_c, current, solved, mixed, cols, rows_ref,
):
    width = update.shape[1]
    panels = factor.shape[1] // width
    eye = (
        lax.broadcasted_iota(jnp.int32, (width, width), 0)
        == lax.broadcasted_iota(jnp.int32, (width, width), 1)
    ).astype(F32)
    current[...] = update[...]
    solved[...] = first[...]
    sums[...] = jnp.zeros(sums.shape, F32)
    for p in range(panels):
        columns = slice(p * width, (p + 1) * width)
        g = solved[...]
        gram_l[...] = eye + mm_nt(g, g)
        gram_c[...] = eye + mm_tn(g, g)
        mixed[...] = factor[:, columns] + mm_nt(current[...], g)
        current[...] = current[...] - mm(factor[:, columns], g)
        if p == 0:
            solved[...] = second[...] - mm(carried[...], g)
        both_inverses([gram_l, gram_c], [inv_l, inv_c], cols, rows_ref)
        cols_out = mm_nt(mixed[...], inv_l[...])
        new_factor[:, columns] = cols_out
        squares = jnp.sum(cols_out * cols_out, axis=0, keepdims=True)
        for c in range(width // N):
            sums[p * (width // N) + c : p * (width // N) + c + 1, :] = squares[:, c * N : (c + 1) * N]
        current[...] = mm_nt(current[...], inv_c[...])
        if p == 0:
            solved[...] = mm_nt(solved[...], inv_c[...])
    new_update[...] = current[...]


def masks_of(rows, cols):
    core = cols if rows > 1 else 0
    others = []
    bit = 1
    while bit < cols:
        others.append(bit if bit < 4 else bit | (bit >> 1))
        bit *= 2
    bit = 2 * cols
    while bit < rows * cols:
        others.append(bit)
        bit *= 2
    return core, others


def spread(held, core, others, my_index, total):
    half = held.shape[0] // 2
    mine = jnp.where((my_index & core) == 0, held[:half], held[half:])
    sent = lax.ppermute(held[half:], AXES, [(0, core), (1, 1 | core)])
    part = jnp.where(my_index < 2, held[:half], sent)
    steps = others[1:]
    turned = steps[1:] + steps[:1]
    seen = [{0, 1}, {core, 1 | core}]
    for step in range(len(steps)):
        pairs = []
        for side, order in ((0, steps), (1, turned)):
            new = {(d, d ^ order[step]) for d in seen[side]}
            pairs += sorted(new)
            seen[side] |= {d for _, d in new}
        got = lax.ppermute(part, AXES, pairs)
        target = jnp.zeros((), bool)
        for _, d in pairs:
            target = target | (my_index == d)
        part = jnp.where(target, got, part)
    other = lax.ppermute(part, AXES, [(d, d ^ 1) for d in range(total)])
    odd = (my_index & 1) == 1
    both = jnp.concatenate([jnp.where(odd, other, part), jnp.where(odd, part, other)], axis=0)
    swapped = lax.ppermute(both, AXES, [(d, d ^ core) for d in range(total)])
    south = (my_index & core) != 0
    a, b = jnp.where(south, swapped, both), jnp.where(south, both, swapped)
    return (
        jnp.concatenate([a[:half], b[:half]], axis=0),
        jnp.concatenate([a[half:], b[half:]], axis=0),
    )


def on_device(factor, update):
    rows, cols_count = lax.axis_size("row"), lax.axis_size("col")
    total = rows * cols_count
    my_index = lax.axis_index(AXES)
    tile, wide = factor.shape[1], factor.shape[2]
    width = update.shape[2]
    panels = wide // width
    flat_factor = factor.reshape(tile, wide)
    flat_update = update.reshape(tile, width)
    square = jax.ShapeDtypeStruct((width, width), F32)
    vmem = pl.BlockSpec(memory_space=pltpu.VMEM)
    scratch = [pltpu.VMEM((2, 2, T * T, N), F32), pltpu.VMEM((2, 2, T, N), F32)]
    solved, carried = pl.pallas_call(
        solve_kernel,
        out_shape=(square, square),
        in_specs=[pl.BlockSpec(memory_space=pltpu.SMEM), vmem, vmem],
        out_specs=(vmem, vmem),
        scratch_shapes=[pltpu.VMEM((width, width), F32)] + scratch,
        name="solve",
    )(jnp.minimum(my_index, panels - 1).reshape(1), flat_factor, flat_update)
    core, others = masks_of(rows, cols_count)
    first, second = spread(solved, core, others, my_index, total)
    _, carried = spread(carried, core, others, my_index, total)
    big = lambda: pltpu.VMEM((width, width), F32)
    new_factor, new_update, sums = pl.pallas_call(
        update_kernel,
        out_shape=(
            jax.ShapeDtypeStruct((tile, wide), F32),
            jax.ShapeDtypeStruct((tile, width), F32),
            jax.ShapeDtypeStruct((T, N), F32),
        ),
        in_specs=[vmem] * 5,
        out_specs=(vmem,) * 3,
        scratch_shapes=[big() for _ in range(7)] + scratch,
        name="update",
    )(flat_factor, flat_update, first, second, carried)
    copies = jnp.broadcast_to(sums[None], (total, T, N)).reshape(total * T, N)
    gathered = lax.all_to_all(copies, AXES, 0, 0, tiled=True)
    squares = jnp.sum(gathered.reshape(total, T, N), axis=0)[: wide // N].reshape(wide)
    column_scale = jnp.sqrt(squares / (tile * total) + 1e-06)
    return (new_factor.reshape(factor.shape), new_update.reshape(update.shape), column_scale)


def solution(mesh):
    return jax.shard_map(
        on_device,
        mesh=mesh,
        in_specs=(P(None, AXES, None), P(None, AXES, None)),
        out_specs=(P(None, AXES, None), P(None, AXES, None), P()),
        check_vma=False,
    )
```

time: 630 us -> 83.5 us (0.13)
  waiting for transfers between devices: 404 us -> 11.8 us
  other arithmetic: 133 us -> 3.05 us
  Pallas kernels: 0 us -> 33.7 us
  blocking collectives: 39 us -> 15.8 us
  starting transfers between devices: 0.08 us -> 16.1 us
  local copies, waits for them, and re-layouts: 16.1 us -> 1.73 us
  matrix products: 13.8 us -> 0 us
  between operations: 14.4 us -> 0.99 us
  loops' own time: 7.45 us -> 0 us
    psum x2 -> x0, waiting for transfers between devices: 404 us -> none  [broadcast(): return lax.psum(jnp.where(mine, array, jnp.zeros_like(array)), axis)]
    another operation x19 -> x0, other arithmetic: 128 us -> none  [the longest x6 34.1 us: panel_terms(): diag_new = jnp.linalg.cholesky(gram_matrix)]
    psum x1 -> x0, blocking collectives: 39 us -> none  [on_device(): squares.append(lax.psum(local_squares, ('row', 'col')))]
    pallas_call x0 -> x2, Pallas kernels: none -> 33.7 us  [the longest x1 25.4 us: on_device(): pl.pallas_call(update_kernel, out_shape=(jax.ShapeDtypeStruct((tile, wide...]
    ppermute x0 -> x12, starting transfers between devices: none -> 16.1 us  [the longest x6 9.27 us: spread(): got = lax.ppermute(part, AXES, pairs)]
    all_to_all x0 -> x1, blocking collectives: none -> 15.8 us  [on_device(): gathered = lax.all_to_all(copies, AXES, 0, 0, tiled=True)]
    another operation x30 -> x0, local copies, waits for them, and re-layouts: 12.4 us -> none  [the longest x10 4.05 us: panel_terms(): lax.linalg.triangular_solve(diag_new, block_factor, left_side=True, lower...]
    ppermute x0 -> x12, waiting for transfers between devices: none -> 11.8 us  [the longest x2 5.69 us: spread(): other = lax.ppermute(part, AXES, [(d, d ^ 1) for d in range(total)])]
  transfers between devices with their start and end apart: 2 -> 12, of which waited for: 2 -> 8; matrix products, arithmetic and copies ran while one was open for 0% -> 1% of each run, Pallas kernels for 0% -> 0%
where the time goes in v1:
time: 83.5 us; the launch traced here: 83.2 us
  Pallas kernels  33.7 us (40%)
  starting transfers between devices  16.1 us (19%)
  blocking collectives  15.8 us (19%)
  waiting for transfers between devices  11.8 us (14%)
  other arithmetic  3.05 us (4%)
  local copies, waits for them, and re-layouts  1.73 us (2%)
  between operations  0.99 us (1%)
    pallas_call x1, Pallas kernels, on_device(): pl.pallas_call(update_kernel, out_shape=(jax.ShapeDtypeStruct((tile, wide...  25.4 us
    all_to_all x1, blocking collectives, on_device(): gathered = lax.all_to_all(copies, AXES, 0, 0, tiled=True)  15.8 us
    ppermute x6, starting transfers between devices, spread(): got = lax.ppermute(part, AXES, pairs)  9.27 us
    pallas_call x1, Pallas kernels, on_device(): pl.pallas_call(solve_kernel, out_shape=(square, square), in_specs=[pl.Blo...  8.31 us
    ppermute x2, waiting for transfers between devices, spread(): other = lax.ppermute(part, AXES, [(d, d ^ 1) for d in range(total)])  5.69 us
    ppermute x6, waiting for transfers between devices, spread(): got = lax.ppermute(part, AXES, pairs)  5.36 us
    ppermute x2, starting transfers between devices, spread(): sent = lax.ppermute(held[half:], AXES, [(0, core), (1, 1 | core)])  3.7 us
    ppermute x2, starting transfers between devices, spread(): other = lax.ppermute(part, AXES, [(d, d ^ 1) for d in range(total)])  2.96 us
  transfers between devices with their start and end apart: 12, of which 8 were waited for; matrix products, arithmetic and copies ran while one was open for 1% of the time, Pallas kernels for 0%

profile of v1, /device:TPU:0, one launch (start us, length us, event | category | flops | bytes accessed | tf_op | source)
XLA Modules:
  0.0 83.2 jit_solution(9633428678459228994)
XLA Ops:
  0.6 8.3 %solve.1 = (f32[256,256]{1,0:T(8,128)}, f32[256,256]{1,0:T(8,128)}) custom-call(s32[1]{0:T(128)} %bitcast.2.mine, f32[256,512]{1,0:T(8,128)} %bitcast.7, f32[256,256]{1,0:T(8,128)} %bitcast.9), custom_call_target="tpu_custom_call" | custom-call | tf_op jit(solution)/shard_map/solve/pallas_call | solution.py:247
  9.0 1.0 %slice.40 = f32[128,256]{1,0:T(8,128)S(1)} slice(f32[256,256]{1,0:T(8,128)} %get-tuple-element.9), slice={[128:256], [0:256]} | slice | bytes 262144 | tf_op jit(solution)/shard_map/slice | solution.py:207
  9.9 2.4 %collective-permute-start.6 = (f32[128,256]{1,0:T(8,128)S(1)}, f32[128,256]{1,0:T(8,128)S(1)}, u32[]{:S(2)}, u32[]{:S(2)}) collective-permute-start(f32[128,256]{1,0:T(8,128)S(1)} %slice.40), channel_id=1, source_target_pairs={{0,8},{1,9}} | collective-permute-start | bytes 393224 | tf_op jit(solution)/shard_map/ppermute | solution.py:207
  12.4 1.3 %collective-permute-start = (f32[128,256]{1,0:T(8,128)S(1)}, f32[128,256]{1,0:T(8,128)S(1)}, u32[]{:S(2)}, u32[]{:S(2)}) collective-permute-start(f32[128,256]{1,0:T(8,128)S(1)} %slice.34), channel_id=1, source_target_pairs={{0,8},{1,9}} | collective-permute-start | bytes 393224 | tf_op jit(solution)/shard_map/ppermute | solution.py:207
  13.9 2.6 %collective-permute-start.7 = (f32[128,256]{1,0:T(8,128)S(1)}, f32[128,256]{1,0:T(8,128)S(1)}, u32[]{:S(2)}, u32[]{:S(2)}) collective-permute-start(f32[128,256]{1,0:T(8,128)S(1)} %slice_select_fusion), channel_id=1, source_target_pairs={{0,2},{1,3},{8,14},{9,15}} | collective-permute-start | bytes 393224 | tf_op jit(solution)/shard_map/ppermute | solution.py:218
  16.5 1.3 %collective-permute-start.1 = (f32[128,256]{1,0:T(8,128)S(1)}, f32[128,256]{1,0:T(8,128)S(1)}, u32[]{:S(2)}, u32[]{:S(2)}) collective-permute-start(f32[128,256]{1,0:T(8,128)S(1)} %slice_select_fusion.1), channel_id=1, source_target_pairs={{0,2},{1,3},{8,14},{9,15}} | collective-permute-start | bytes 393224 | tf_op jit(solution)/shard_map/ppermute | solution.py:218
  17.8 1.6 %collective-permute-done.7 = f32[128,256]{1,0:T(8,128)S(1)} collective-permute-done((f32[128,256]{1,0:T(8,128)S(1)}, f32[128,256]{1,0:T(8,128)S(1)}, u32[]{:S(2)}, u32[]{:S(2)}) %collective-permute-start.7) | collective-permute-done | bytes 131104 | tf_op jit(solution)/shard_map/ppermute | solution.py:218
  19.5 1.3 %collective-permute-start.8 = (f32[128,256]{1,0:T(8,128)S(1)}, f32[128,256]{1,0:T(8,128)S(1)}, u32[]{:S(2)}, u32[]{:S(2)}) collective-permute-start(f32[128,256]{1,0:T(8,128)S(1)} %broadcast_select_fusion.2), channel_id=1, source_target_pairs={{0,6},{1,7},{2,4},{3,5},{8,24},{9,25},{14,30},{15,31}} | collective-permute-start | bytes 393224 | tf_op jit(solution)/shard_map/ppermute | solution.py:218
  20.8 1.5 %collective-permute-done.1 = f32[128,256]{1,0:T(8,128)S(1)} collective-permute-done((f32[128,256]{1,0:T(8,128)S(1)}, f32[128,256]{1,0:T(8,128)S(1)}, u32[]{:S(2)}, u32[]{:S(2)}) %collective-permute-start.1) | collective-permute-done | bytes 131104 | tf_op jit(solution)/shard_map/ppermute | solution.py:218
  22.3 1.3 %collective-permute-start.2 = (f32[128,256]{1,0:T(8,128)S(1)}, f32[128,256]{1,0:T(8,128)S(1)}, u32[]{:S(2)}, u32[]{:S(2)}) collective-permute-start(f32[128,256]{1,0:T(8,128)S(1)} %broadcast_select_fusion.3), channel_id=1, source_target_pairs={{0,6},{1,7},{2,4},{3,5},{8,24},{9,25},{14,30},{15,31}} | collective-permute-start | bytes 393224 | tf_op jit(solution)/shard_map/ppermute | solution.py:218
  23.6 1.0 %collective-permute-done.8 = f32[128,256]{1,0:T(8,128)S(1)} collective-permute-done((f32[128,256]{1,0:T(8,128)S(1)}, f32[128,256]{1,0:T(8,128)S(1)}, u32[]{:S(2)}, u32[]{:S(2)}) %collective-permute-start.8) | collective-permute-done | bytes 131104 | tf_op jit(solution)/shard_map/ppermute | solution.py:218
  24.6 1.3 %collective-permute-start.9 = (f32[128,256]{1,0:T(8,128)S(1)}, f32[128,256]{1,0:T(8,128)S(1)}, u32[]{:S(2)}, u32[]{:S(2)}) collective-permute-start(f32[128,256]{1,0:T(8,128)S(1)} %broadcast_select_fusion.4), channel_id=1, source_target_pairs={{0,16},{1,17},{2,18},{3,19},{4,20},{5,21},{6,22},{7,23},{8,10},{9,... | collective-permute-start | bytes 393224 | tf_op jit(solution)/shard_map/ppermute | solution.py:218
  26.1 1.5 %collective-permute-start.3 = (f32[128,256]{1,0:T(8,128)S(1)}, f32[128,256]{1,0:T(8,128)S(1)}, u32[]{:S(2)}, u32[]{:S(2)}) collective-permute-start(f32[128,256]{1,0:T(8,128)S(1)} %broadcast_select_fusion.5), channel_id=1, source_target_pairs={{0,16},{1,17},{2,18},{3,19},{4,20},{5,21},{6,22},{7,23},{8,10},{9,... | collective-permute-start | bytes 393224 | tf_op jit(solution)/shard_map/ppermute | solution.py:218
  27.6 1.1 %collective-permute-done.9 = f32[128,256]{1,0:T(8,128)S(1)} collective-permute-done((f32[128,256]{1,0:T(8,128)S(1)}, f32[128,256]{1,0:T(8,128)S(1)}, u32[]{:S(2)}, u32[]{:S(2)}) %collective-permute-start.9) | collective-permute-done | bytes 131104 | tf_op jit(solution)/shard_map/ppermute | solution.py:218
  28.7 1.6 %collective-permute-start.10 = (f32[128,256]{1,0:T(8,128)S(1)}, f32[128,256]{1,0:T(8,128)S(1)}, u32[]{:S(2)}, u32[]{:S(2)}) collective-permute-start(f32[128,256]{1,0:T(8,128)S(1)} %broadcast_select_fusion.6), channel_id=1, source_target_pairs={{0,1},{1,0},{2,3},{3,2},{4,5},{5,4},{6,7},{7,6},{8,9},{9,8},{10,11... | collective-permute-start | bytes 393224 | tf_op jit(solution)/shard_map/ppermute | solution.py:223
  30.3 1.4 %collective-permute-start.4 = (f32[128,256]{1,0:T(8,128)S(1)}, f32[128,256]{1,0:T(8,128)S(1)}, u32[]{:S(2)}, u32[]{:S(2)}) collective-permute-start(f32[128,256]{1,0:T(8,128)S(1)} %broadcast_select_fusion.7), channel_id=1, source_target_pairs={{0,1},{1,0},{2,3},{3,2},{4,5},{5,4},{6,7},{7,6},{8,9},{9,8},{10,11... | collective-permute-start | bytes 393224 | tf_op jit(solution)/shard_map/ppermute | solution.py:223
  31.7 3.4 %collective-permute-done.10 = f32[128,256]{1,0:T(8,128)S(1)} collective-permute-done((f32[128,256]{1,0:T(8,128)S(1)}, f32[128,256]{1,0:T(8,128)S(1)}, u32[]{:S(2)}, u32[]{:S(2)}) %collective-permute-start.10) | collective-permute-done | bytes 131104 | tf_op jit(solution)/shard_map/ppermute | solution.py:223
  35.2 2.2 %collective-permute-done.4 = f32[128,256]{1,0:T(8,128)S(1)} collective-permute-done((f32[128,256]{1,0:T(8,128)S(1)}, f32[128,256]{1,0:T(8,128)S(1)}, u32[]{:S(2)}, u32[]{:S(2)}) %collective-permute-start.4) | collective-permute-done | bytes 131104 | tf_op jit(solution)/shard_map/ppermute | solution.py:223
  37.6 0.7 pad_maximum_fusion.4.carried
  38.4 0.8 collective-permute-done.5
  39.2 0.7 pad_maximum_fusion.3.second
  39.9 0.7 pad_maximum_fusion.2.first
  40.7 25.4 %update.1 = (f32[256,512]{1,0:T(8,128)}, f32[256,256]{1,0:T(8,128)}, f32[8,128]{1,0:T(8,128)}) custom-call(f32[256,512]{1,0:T(8,128)} %bitcast.8, f32[256,256]{1,0:T(8,128)} %bitcast.10, f32[256,256]{1,0:T(8,128)} %pad_maximum_fusion.2.first, f32[256,256]{1,0:T(8,128)} %pad_maximum_fusion.3.second, f32[256,256]{1,0:T(8,128)} %pad_maximum_fusion.4.carried), custom_call_target="tpu_custom_call" | custom-call | tf_op jit(solution)/shard_map/update/pallas_call | solution.py:259
  66.8 15.8 %all_to_all.6 = f32[32,8,128]{2,1,0:T(8,128)S(1)} all-to-all(f32[32,8,128]{2,1,0:T(8,128)S(1)} %broadcast_in_dim.2), channel_id=1, replica_groups=mesh['row'=4,'col'=8] {'row','col'}, dimensions={0} | all-to-all | bytes 262144 | tf_op jit(solution)/shard_map/all_to_all | solution.py:272
  (30 shorter events, 2.0 us)
Async XLA Ops:
  8.9 3.4 %copy-start = (f32[256,256]{1,0:T(8,128)S(1)}, f32[256,256]{1,0:T(8,128)}, u32[]{:S(2)}) copy-start(f32[256,256]{1,0:T(8,128)} %get-tuple-element.8) | copy-start | bytes 786436
  8.9 4.9 %copy-start.1 = (f32[256,256]{1,0:T(8,128)S(1)}, f32[256,256]{1,0:T(8,128)}, u32[]{:S(2)}) copy-start(f32[256,256]{1,0:T(8,128)} %get-tuple-element.9) | copy-start | bytes 786436
  9.9 3.9 %collective-permute-start.6 = (f32[128,256]{1,0:T(8,128)S(1)}, f32[128,256]{1,0:T(8,128)S(1)}, u32[]{:S(2)}, u32[]{:S(2)}) collective-permute-start(f32[128,256]{1,0:T(8,128)S(1)} %slice.40), channel_id=1, source_target_pairs={{0,8},{1,9}} | collective-permute-start | bytes 393224 | tf_op jit(solution)/shard_map/ppermute | solution.py:207
  12.4 4.1 %collective-permute-start = (f32[128,256]{1,0:T(8,128)S(1)}, f32[128,256]{1,0:T(8,128)S(1)}, u32[]{:S(2)}, u32[]{:S(2)}) collective-permute-start(f32[128,256]{1,0:T(8,128)S(1)} %slice.34), channel_id=1, source_target_pairs={{0,8},{1,9}} | collective-permute-start | bytes 393224 | tf_op jit(solution)/shard_map/ppermute | solution.py:207
  13.9 5.6 %collective-permute-start.7 = (f32[128,256]{1,0:T(8,128)S(1)}, f32[128,256]{1,0:T(8,128)S(1)}, u32[]{:S(2)}, u32[]{:S(2)}) collective-permute-start(f32[128,256]{1,0:T(8,128)S(1)} %slice_select_fusion), channel_id=1, source_target_pairs={{0,2},{1,3},{8,14},{9,15}} | collective-permute-start | bytes 393224 | tf_op jit(solution)/shard_map/ppermute | solution.py:218
  16.5 5.7 %collective-permute-start.1 = (f32[128,256]{1,0:T(8,128)S(1)}, f32[128,256]{1,0:T(8,128)S(1)}, u32[]{:S(2)}, u32[]{:S(2)}) collective-permute-start(f32[128,256]{1,0:T(8,128)S(1)} %slice_select_fusion.1), channel_id=1, source_target_pairs={{0,2},{1,3},{8,14},{9,15}} | collective-permute-start | bytes 393224 | tf_op jit(solution)/shard_map/ppermute | solution.py:218
  19.5 5.1 %collective-permute-start.8 = (f32[128,256]{1,0:T(8,128)S(1)}, f32[128,256]{1,0:T(8,128)S(1)}, u32[]{:S(2)}, u32[]{:S(2)}) collective-permute-start(f32[128,256]{1,0:T(8,128)S(1)} %broadcast_select_fusion.2), channel_id=1, source_target_pairs={{0,6},{1,7},{2,4},{3,5},{8,24},{9,25},{14,30},{15,31}} | collective-permute-start | bytes 393224 | tf_op jit(solution)/shard_map/ppermute | solution.py:218
  22.3 3.8 %collective-permute-start.2 = (f32[128,256]{1,0:T(8,128)S(1)}, f32[128,256]{1,0:T(8,128)S(1)}, u32[]{:S(2)}, u32[]{:S(2)}) collective-permute-start(f32[128,256]{1,0:T(8,128)S(1)} %broadcast_select_fusion.3), channel_id=1, source_target_pairs={{0,6},{1,7},{2,4},{3,5},{8,24},{9,25},{14,30},{15,31}} | collective-permute-start | bytes 393224 | tf_op jit(solution)/shard_map/ppermute | solution.py:218
  24.6 4.1 %collective-permute-start.9 = (f32[128,256]{1,0:T(8,128)S(1)}, f32[128,256]{1,0:T(8,128)S(1)}, u32[]{:S(2)}, u32[]{:S(2)}) collective-permute-start(f32[128,256]{1,0:T(8,128)S(1)} %broadcast_select_fusion.4), channel_id=1, source_target_pairs={{0,16},{1,17},{2,18},{3,19},{4,20},{5,21},{6,22},{7,23},{8,10},{9,... | collective-permute-start | bytes 393224 | tf_op jit(solution)/shard_map/ppermute | solution.py:218
  26.1 4.2 %collective-permute-start.3 = (f32[128,256]{1,0:T(8,128)S(1)}, f32[128,256]{1,0:T(8,128)S(1)}, u32[]{:S(2)}, u32[]{:S(2)}) collective-permute-start(f32[128,256]{1,0:T(8,128)S(1)} %broadcast_select_fusion.5), channel_id=1, source_target_pairs={{0,16},{1,17},{2,18},{3,19},{4,20},{5,21},{6,22},{7,23},{8,10},{9,... | collective-permute-start | bytes 393224 | tf_op jit(solution)/shard_map/ppermute | solution.py:218
  28.7 6.4 %collective-permute-start.10 = (f32[128,256]{1,0:T(8,128)S(1)}, f32[128,256]{1,0:T(8,128)S(1)}, u32[]{:S(2)}, u32[]{:S(2)}) collective-permute-start(f32[128,256]{1,0:T(8,128)S(1)} %broadcast_select_fusion.6), channel_id=1, source_target_pairs={{0,1},{1,0},{2,3},{3,2},{4,5},{5,4},{6,7},{7,6},{8,9},{9,8},{10,11... | collective-permute-start | bytes 393224 | tf_op jit(solution)/shard_map/ppermute | solution.py:223
  30.3 7.2 %collective-permute-start.4 = (f32[128,256]{1,0:T(8,128)S(1)}, f32[128,256]{1,0:T(8,128)S(1)}, u32[]{:S(2)}, u32[]{:S(2)}) collective-permute-start(f32[128,256]{1,0:T(8,128)S(1)} %broadcast_select_fusion.7), channel_id=1, source_target_pairs={{0,1},{1,0},{2,3},{3,2},{4,5},{5,4},{6,7},{7,6},{8,9},{9,8},{10,11... | collective-permute-start | bytes 393224 | tf_op jit(solution)/shard_map/ppermute | solution.py:223
  35.2 2.5 %collective-permute-start.11 = (f32[256,256]{1,0:T(8,128)S(1)}, f32[256,256]{1,0:T(8,128)S(1)}, u32[]{:S(2)}, u32[]{:S(2)}) collective-permute-start(f32[256,256]{1,0:T(8,128)S(1)} %pad_maximum_fusion), channel_id=1, source_target_pairs={{0,8},{1,9},{2,10},{3,11},{4,12},{5,13},{6,14},{7,15},{8,0},{9,1},... | collective-permute-start | bytes 786440 | tf_op jit(solution)/shard_map/ppermute | solution.py:226
  37.5 1.6 %collective-permute-start.5 = (f32[256,256]{1,0:T(8,128)S(1)}, f32[256,256]{1,0:T(8,128)S(1)}, u32[]{:S(2)}, u32[]{:S(2)}) collective-permute-start(f32[256,256]{1,0:T(8,128)S(1)} %pad_maximum_fusion.1), channel_id=1, source_target_pairs={{0,8},{1,9},{2,10},{3,11},{4,12},{5,13},{6,14},{7,15},{8,0},{9,1},... | collective-permute-start | bytes 786440 | tf_op jit(solution)/shard_map/ppermute | solution.py:226

commit v2 on v0

v2 whole, which is shorter than its diff:
```python
import jax
import jax.numpy as jnp
from jax import lax
from jax.experimental import pallas as pl
from jax.experimental.pallas import tpu as pltpu
from jax.sharding import PartitionSpec as P

T = 8
N = 128
H = N // 2
NB = H // T
AXES = ("row", "col")
F32 = jnp.float32
HI = lax.Precision.HIGHEST

def dot(a, b, ca, cb):
    return lax.dot_general(a, b, (((ca,), (cb,)), ((), ())), precision=HI, preferred_element_type=F32)

def mm(a, b):
    return dot(a, b, 1, 0)

def mm_nt(a, b):
    return dot(a, b, 1, 1)

def mm_tn(a, b):
    return dot(a, b, 0, 0)

def half_masks():
    lane = lax.broadcasted_iota(jnp.int32, (T, N), 1)
    sub = lax.broadcasted_iota(jnp.int32, (T, N), 0)
    left = lane < H
    return jnp.where(left, lane, lane - H), sub, jnp.where(left, 0, H)

def pick(x, base, c):
    return jnp.take_along_axis(x, base + c, axis=1, mode="promise_in_bounds")

def row_bcast(ref, row):
    return jnp.broadcast_to(ref[row : row + 1, :], (T, N))

def assemble(rows, k, col, sub):
    tile = rows[T - 1]
    for j in range(T - 2, -1, -1):
        tile = jnp.where(sub <= j, rows[j], tile)
    return jnp.where(col <= sub + k, tile, 0.0)

def chol_leaf(mat, sc, sl, sr):
    col, sub, base = half_masks()
    mat = list(mat)
    out = []
    own = [pick(mat[0], base, j) for j in range(T)]
    for b in range(NB):
        k = b * T
        inside = (col >= k) & (col < k + T)
        unit = (col == sub + k).astype(F32)
        cs, ls, rs = sc.at[b % 2], sl.at[b % 2], sr.at[b % 2]
        for j in range(T):
            cs[j * T : (j + 1) * T, :] = own[j]
        rs[...] = jnp.where(inside, unit, mat[b])
        a = {(i, j): row_bcast(cs, j * T + i) for j in range(T) for i in range(j, T)}
        r = [row_bcast(rs, j) for j in range(T)]
        below = range(b + 1, NB)
        c = {t: [pick(mat[t], base, k + j) for j in range(T)] for t in below}
        if b < NB - 1:
            own = [pick(mat[b + 1], base, k + T + j) for j in range(T)]
        acc = {t: jnp.where(inside, 0.0, mat[t]) for t in below}
        for j in range(T):
            scale = lax.rsqrt(a[j, j])
            low = {i: a[i, j] * scale for i in range(j + 1, T)}
            for i in range(j + 1, T):
                for i2 in range(j + 1, i + 1):
                    a[i, i2] = a[i, i2] - low[i] * low[i2]
            r[j] = r[j] * scale
            for i in range(j + 1, T):
                r[i] = r[i] - low[i] * r[j]
            for t in below:
                c[t][j] = c[t][j] * scale
                for i in range(j + 1, T):
                    c[t][i] = c[t][i] - low[i] * c[t][j]
                acc[t] = acc[t] - c[t][j] * r[j]
            if b < NB - 1:
                ls[j * T : (j + 1) * T, :] = c[b + 1][j]
                for i in range(T):
                    own[i] = own[i] - c[b + 1][j] * row_bcast(ls, j * T + i)
        out.append(assemble(r, k, col, sub))
        for t in below:
            mat[t] = acc[t]
    return out

def tri_leaf(mats, scs, srs):
    col, sub, base = half_masks()
    mats = [list(m) for m in mats]
    outs = [[] for _ in mats]
    picks = []
    for mat, sc in zip(mats, scs):
        picks.append([{t: [pick(mat[t], base, b * T + j) for j in range(T)] for t in range(b, NB)} for b in range(NB)])
        for b in range(NB):
            for j in range(T):
                sc[b, j * T : (j + 1) * T, :] = picks[-1][b][b][j]
    mats = [[jnp.zeros((T, N), F32) for _ in m] for m in mats]
    for b in range(NB):
        k = b * T
        inside = (col >= k) & (col < k + T)
        unit = (col == sub + k).astype(F32)
        for q, mat in enumerate(mats):
            cs, rs = scs[q].at[b], srs[q].at[b % 2]
            rs[...] = jnp.where(inside, unit, mat[b])
            r = [row_bcast(rs, j) for j in range(T)]
            for j in range(T):
                r[j] = r[j] * (1.0 / row_bcast(cs, j * T + j))
                for i in range(j + 1, T):
                    r[i] = r[i] - row_bcast(cs, j * T + i) * r[j]
            outs[q].append(assemble(r, k, col, sub))
            for t in range(b + 1, NB):
                for j in range(T):
                    mat[t] = mat[t] - picks[q][b][t][j] * r[j]
    return outs

def split_halves(x):
    lane = lax.broadcasted_iota(jnp.int32, x.shape, 1)
    return jnp.concatenate([jnp.where(lane < H, x, 0.0), jnp.where(lane < H, 0.0, x)], axis=0)

def pack(first, second):
    lane = lax.broadcasted_iota(jnp.int32, (first.shape[0], N), 1)
    out = []
    for c in range(0, first.shape[1], N):
        x, y = first[:, c : c + N], second[:, c : c + N]
        out.append(jnp.where(lane < H, x, pltpu.roll(y, H, 1)))
        out.append(jnp.where(lane < H, pltpu.roll(x, H, 1), y))
    return out

def tiles_of(ref, r0, c0):
    return [ref[r0 + t * T : r0 + (t + 1) * T, c0 : c0 + N] for t in range(NB)]

def chol_inverse_pair(gram, inv, tmp, sc, sl, sr):
    n = gram.shape[0]
    nb = n // H
    low = {}
    for d in range(nb):
        at = slice(d * H, (d + 1) * H)
        for t, tile in enumerate(chol_leaf(tiles_of(gram, d * H, d * N), sc, sl, sr)):
            inv[d * H + t * T : d * H + (t + 1) * T, d * N : (d + 1) * N] = tile
        w = inv[at, d * N : (d + 1) * N]
        if d < nb - 1:
            rest = slice((d + 1) * H, n)
            tmp[rest, d * N : (d + 1) * N] = mm_nt(gram[rest, d * N : (d + 1) * N], split_halves(w))
            for e in range(d + 1, nb):
                rows = slice(e * H, n)
                cols = slice(e * N, (e + 1) * N)
                gram[rows, cols] = gram[rows, cols] - mm_nt(
                    tmp[rows, d * N : (d + 1) * N], split_halves(tmp[e * H : (e + 1) * H, d * N : (d + 1) * N])
                )
        for c in range(d):
            cols = slice(c * N, (c + 1) * N)
            part = None
            for e in range(c, d):
                term = mm(tmp[at, e * N : (e + 1) * N], split_halves(inv[e * H : (e + 1) * H, cols]))
                part = term if part is None else part + term
            inv[at, cols] = -mm(w, split_halves(part))

def unpack(inv, first, second):
    n = inv.shape[0]
    lane = lax.broadcasted_iota(jnp.int32, (n, N), 1)
    row = lax.broadcasted_iota(jnp.int32, (n, N), 0)
    for c in range(0, n, N):
        x, y = inv[:, 2 * c : 2 * c + N], inv[:, 2 * c + N : 2 * c + 2 * N]
        x = jnp.where(row >= c, x, 0.0)
        y = jnp.where(row >= c + H, y, 0.0)
        first[:, c : c + N] = jnp.where(lane < H, x, pltpu.roll(y, H, 1))
        second[:, c : c + N] = jnp.where(lane < H, pltpu.roll(x, H, 1), y)

def tri_inverse(block, inverse, scs, srs):
    n = block.shape[0]
    lane = lax.broadcasted_iota(jnp.int32, (T, N), 1)
    mats = []
    for c in range(0, n, N):
        mats.append([
            jnp.where(lane < H, block[c + t * T : c + (t + 1) * T, c : c + N], block[c + H + t * T : c + H + (t + 1) * T, c : c + N])
            for t in range(NB)
        ])
    outs = tri_leaf(mats, scs, srs)
    for c, out in zip(range(0, n, N), outs):
        for t, tile in enumerate(out):
            inverse[c + t * T : c + (t + 1) * T, c : c + N] = jnp.where(lane < H, tile, 0.0)
            inverse[c + H + t * T : c + H + (t + 1) * T, c : c + N] = jnp.where(lane < H, 0.0, tile)
    big = lax.broadcasted_iota(jnp.int32, (H, N), 1)
    for c in range(0, n, N):
        diag = inverse[c : c + N, c : c + N]
        corner = jnp.where(big < H, block[c + H : c + N, c : c + N], 0.0)
        t1 = mm(corner, diag)
        t2 = mm(diag[H:, :], jnp.concatenate([jnp.zeros((H, N), F32), t1], axis=0))
        inverse[c + H : c + N, c : c + N] = diag[H:, :] - t2


def inverse_kernel(flags, factor, inverse, scs, srs):
    width = inverse.shape[0]
    block = factor.at[:, pl.ds(pl.multiple_of(flags[0] * width, width), width)]
    tri_inverse(block, inverse, [scs.at[q] for q in range(2)], [srs.at[q] for q in range(2)])


def solve_kernel(flags, factor, update, inverse, left, right, rhs):
    width = update.shape[1]
    half = width // 2
    block = factor.at[:, pl.ds(pl.multiple_of(flags[0] * width, width), width)]
    for c in range(0, width, N):
        at = slice(c, c + N)
        inv = inverse[at, at]
        for source, low in ((update, 0), (factor, width)):
            value = source[at, :width]
            if c > 0:
                value = value - mm(block[at, :c], rhs[:c, low : low + width])
            rhs[at, low : low + width] = mm(inv, value)
    for out, low in ((left, 0), (right, half)):
        out[:, :half] = rhs[:, low : low + half]
        out[:, half:] = rhs[:, width + low : width + low + half]


def panel_step(columns, current, g, new_columns, inv_l, inv_c, gram, inv, tmp, sc, sl, sr):
    width = g.shape[0]
    eye = (
        lax.broadcasted_iota(jnp.int32, (width, width), 0)
        == lax.broadcasted_iota(jnp.int32, (width, width), 1)
    ).astype(F32)
    x = g[...]
    for c, part in enumerate(pack(eye + mm_nt(x, x), eye + mm_tn(x, x))):
        gram[:, c * N : (c + 1) * N] = part
    cols = columns[...]
    v = current[...]
    new_columns[...] = cols + mm_nt(v, x)
    current[...] = v - mm(cols, x)
    chol_inverse_pair(gram, inv, tmp, sc, sl, sr)
    unpack(inv, inv_l, inv_c)
    new_columns[...] = mm_nt(new_columns[...], inv_l[...])
    current[...] = mm_nt(current[...], inv_c[...])


def update_kernel(
    flags, factor, update, own, other, own_swapped, other_swapped,
    new_factor, current, copies, g, x, inv_l, inv_c, *rest,
):
    width = g.shape[0]
    half = width // 2
    south = flags[1] == 1
    odd = flags[2] == 1

    def halves(low, swap):
        at = slice(low, low + half)
        here = jnp.where(odd != swap, other[:, at], own[:, at])
        there = jnp.where(odd != swap, other_swapped[:, at], own_swapped[:, at])
        return jnp.where(south, there, here), jnp.where(south, here, there)

    g[:, :half], g[:, half:] = halves(0, False)
    y = jnp.concatenate(halves(half, True), axis=1)
    x[...] = jnp.concatenate(halves(0, True), axis=1) - mm(y, g[...])
    current[...] = update[...]
    panel_step(factor.at[:, :width], current, g, new_factor.at[:, :width], inv_l, inv_c, *rest)
    x[...] = mm_nt(x[...], inv_c[...])
    panel_step(factor.at[:, width:], current, x, new_factor.at[:, width:], inv_l, inv_c, *rest)
    squares = jnp.sum(new_factor[...] * new_factor[...], axis=0, keepdims=True)
    sub = lax.broadcasted_iota(jnp.int32, (T, N), 0)
    tile = jnp.zeros((T, N), F32)
    for c in range(squares.shape[1] // N):
        tile = jnp.where(sub == c, squares[:, c * N : (c + 1) * N], tile)
    for d in range(copies.shape[0] // T):
        copies[d * T : (d + 1) * T, :] = tile


def masks_of(rows, cols):
    bits = lambda low, high: [1 << b for b in range(high.bit_length() - 2, low.bit_length() - 2, -1)]
    return cols, bits(2, cols) + bits(2 * cols, rows * cols)


def spread(left, right, my_index, core, steps, roots):
    turned = steps[-1:] + steps[:-1]
    sent = lax.ppermute(right, AXES, [(d, d | core) for d in roots])
    part = jnp.where((my_index & core) != 0, sent, left)
    seen = [set(roots), {core | d for d in roots}]
    for step in range(len(steps)):
        pairs = []
        for side, order in ((0, steps), (1, turned)):
            new = {(d, d ^ order[step]) for d in seen[side]}
            pairs += sorted(new)
            seen[side] |= {d for _, d in new}
        came = lax.ppermute(part, AXES, pairs)
        target = jnp.zeros((), bool)
        for _, d in pairs:
            target = target | (my_index == d)
        part = jnp.where(target, came, part)
    return part


def on_device(factor, update):
    rows, cols_count = lax.axis_size("row"), lax.axis_size("col")
    total = rows * cols_count
    my_index = lax.axis_index(AXES)
    tile, wide = factor.shape[1], factor.shape[2]
    width = update.shape[2]
    panels = wide // width
    flat_factor = factor.reshape(tile, wide)
    flat_update = update.reshape(tile, width)
    core, others = masks_of(rows, cols_count)
    panel = jnp.minimum(my_index & ~core, panels - 1)
    flags = jnp.stack([panel, jnp.minimum(my_index & core, 1), my_index & 1]).astype(jnp.int32)
    smem = pl.BlockSpec(memory_space=pltpu.SMEM)
    vmem = pl.BlockSpec(memory_space=pltpu.VMEM)
    shape = lambda *dims: jax.ShapeDtypeStruct(dims, F32)
    work = lambda *dims: pltpu.VMEM(dims, F32)
    limit = pltpu.CompilerParams(vmem_limit_bytes=24 * 2 ** 20)

    blocks = width // N
    inverse = pl.pallas_call(
        inverse_kernel,
        out_shape=shape(width, width),
        in_specs=[smem, vmem],
        out_specs=vmem,
        scratch_shapes=[work(blocks, NB, T * T, N), work(blocks, 2, T, N)],
        compiler_params=limit,
        name="inverse",
    )(flags, flat_factor)
    left, right = pl.pallas_call(
        solve_kernel,
        out_shape=(shape(width, width),) * 2,
        in_specs=[smem] + [vmem] * 3,
        out_specs=(vmem,) * 2,
        scratch_shapes=[work(width, 2 * width)],
        compiler_params=limit,
        name="solve",
    )(flags, flat_factor, flat_update, inverse)
    own = spread(left, right, my_index, core, others, (0, 1))
    partner = [(d, d ^ core) for d in range(total)]
    other = lax.ppermute(own, AXES, [(d, d ^ 1) for d in range(total)])
    own_swapped = lax.ppermute(own, AXES, partner)
    other_swapped = lax.ppermute(other, AXES, partner)
    new_factor, new_update, copies = pl.pallas_call(
        update_kernel,
        out_shape=(shape(tile, wide), shape(tile, width), shape(total * T, N)),
        in_specs=[smem] + [vmem] * 6,
        out_specs=(vmem,) * 3,
        scratch_shapes=[work(width, width)] * 4
        + [work(width, 2 * width)] * 3
        + [work(2, T * T, N), work(2, T * T, N), work(2, T, N)],
        compiler_params=limit,
        cost_estimate=pl.CostEstimate(flops=10 ** 10, bytes_accessed=2 ** 21, transcendentals=0),
        name="update",
    )(flags, flat_factor, flat_update, own, other, own_swapped, other_swapped)
    gathered = lax.all_to_all(copies, AXES, 0, 0, tiled=True)
    squares = jnp.sum(gathered.reshape(total, T, N), axis=0)[: wide // N].reshape(wide)
    column_scale = jnp.sqrt(squares / (tile * total) + 1e-06)
    return (new_factor.reshape(factor.shape), new_update.reshape(update.shape), column_scale)


def solution(mesh):
    return jax.shard_map(
        on_device,
        mesh=mesh,
        in_specs=(P(None, AXES, None), P(None, AXES, None)),
        out_specs=(P(None, AXES, None), P(None, AXES, None), P()),
        check_vma=False,
    )
```

time: 630 us -> 73.2 us (0.12)
  waiting for transfers between devices: 404 us -> 20.4 us
  other arithmetic: 133 us -> 0.84 us
  Pallas kernels: 0 us -> 24.8 us
  blocking collectives: 39 us -> 15.2 us
  local copies, waits for them, and re-layouts: 16.1 us -> 1.05 us
  matrix products: 13.8 us -> 0 us
  between operations: 14.4 us -> 0.83 us
  starting transfers between devices: 0.08 us -> 9.72 us
  loops' own time: 7.45 us -> 0 us
    psum x2 -> x0, waiting for transfers between devices: 404 us -> none  [broadcast(): return lax.psum(jnp.where(mine, array, jnp.zeros_like(array)), axis)]
    another operation x19 -> x1, other arithmetic: 128 us -> 0.08 us  [on_device(): jnp.stack([panel, jnp.minimum(my_index & core, 1), my_index & 1])]
    psum x1 -> x0, blocking collectives: 39 us -> none  [on_device(): squares.append(lax.psum(local_squares, ('row', 'col')))]
    pallas_call x0 -> x3, Pallas kernels: none -> 24.8 us  [the longest x1 20.3 us: on_device(): pl.pallas_call(update_kernel, out_shape=(shape(tile, wide), shape(tile, w...]
    ppermute x0 -> x7, waiting for transfers between devices: none -> 20.4 us  [the longest x3 12.5 us: spread(): came = lax.ppermute(part, AXES, pairs)]
    all_to_all x0 -> x1, blocking collectives: none -> 15.2 us  [on_device(): gathered = lax.all_to_all(copies, AXES, 0, 0, tiled=True)]
    another operation x30 -> x0, local copies, waits for them, and re-layouts: 12.4 us -> none  [the longest x10 4.05 us: panel_terms(): lax.linalg.triangular_solve(diag_new, block_factor, left_side=True, lower...]
    ppermute x0 -> x7, starting transfers between devices: none -> 9.72 us  [the longest x3 6.07 us: spread(): came = lax.ppermute(part, AXES, pairs)]
  transfers between devices with their start and end apart: 2 -> 7, of which waited for: 2 -> 6; matrix products, arithmetic and copies ran while one was open for 0% -> 0% of each run, Pallas kernels for 0% -> 0%
where the time goes in v2:
time: 73.2 us; the launch traced here: 72.9 us
  Pallas kernels  24.8 us (34%)
  waiting for transfers between devices  20.4 us (28%)
  blocking collectives  15.2 us (21%)
  starting transfers between devices  9.72 us (13%)
  local copies, waits for them, and re-layouts  1.05 us (1%)
  other arithmetic  0.84 us (1%)
  between operations  0.83 us (1%)
    pallas_call x1, Pallas kernels, on_device(): pl.pallas_call(update_kernel, out_shape=(shape(tile, wide), shape(tile, w...  20.3 us
    all_to_all x1, blocking collectives, on_device(): gathered = lax.all_to_all(copies, AXES, 0, 0, tiled=True)  15.2 us
    ppermute x3, waiting for transfers between devices, spread(): came = lax.ppermute(part, AXES, pairs)  12.5 us
    ppermute x3, starting transfers between devices, spread(): came = lax.ppermute(part, AXES, pairs)  6.07 us
    ppermute x1, waiting for transfers between devices, on_device(): other = lax.ppermute(own, AXES, [(d, d ^ 1) for d in range(total)])  5.19 us
    pallas_call x1, Pallas kernels, on_device(): pl.pallas_call(inverse_kernel, out_shape=shape(width, width), in_specs=[s...  2.77 us
    ppermute x1, starting transfers between devices, spread(): sent = lax.ppermute(right, AXES, [(d, d | core) for d in roots])  2.41 us
    pallas_call x1, Pallas kernels, on_device(): pl.pallas_call(solve_kernel, out_shape=(shape(width, width),) * 2, in_spe...  1.73 us
  transfers between devices with their start and end apart: 7, of which 6 were waited for; matrix products, arithmetic and copies ran while one was open for 0% of the time, Pallas kernels for 0%

profile of v2, /device:TPU:0, one launch (start us, length us, event | category | flops | bytes accessed | tf_op | source)
XLA Modules:
  0.0 72.9 jit_solution(326826430842423520)
XLA Ops:
  0.6 0.1 pad_add_fusion.flags
  0.7 1.0 %copy-done = f32[1,256,512]{2,1,0:T(8,128)S(1)} copy-done((f32[1,256,512]{2,1,0:T(8,128)S(1)}, f32[1,256,512]{2,1,0:T(8,128)}, u32[]{:S(2)}) %copy-start) | copy-done | bytes 524312
  1.8 2.8 %inverse.1 = f32[256,256]{1,0:T(8,128)S(1)} custom-call(s32[3]{0:T(128)S(1)} %pad_add_fusion.flags, f32[256,512]{1,0:T(8,128)S(1)} %bitcast.10), custom_call_target="tpu_custom_call" | custom-call | tf_op jit(solution)/shard_map/inverse/pallas_call | solution.py:310
  4.5 0.0 copy-done.2
  4.6 1.7 %solve.1 = (f32[256,256]{1,0:T(8,128)S(1)}, f32[256,256]{1,0:T(8,128)S(1)}) custom-call(s32[3]{0:T(128)S(1)} %pad_add_fusion.flags, f32[256,512]{1,0:T(8,128)S(1)} %bitcast.11, f32[256,256]{1,0:T(8,128)S(1)} %bitcast.13, f32[256,256]{1,0:T(8,128)S(1)} %inverse.1), custom_call_target="tpu_custom_call" | custom-call | tf_op jit(solution)/shard_map/solve/pallas_call | solution.py:319
  6.3 2.4 %collective-permute-start = (f32[256,256]{1,0:T(8,128)S(1)}, f32[256,256]{1,0:T(8,128)S(1)}, u32[]{:S(2)}, u32[]{:S(2)}) collective-permute-start(f32[256,256]{1,0:T(8,128)S(1)} %get-tuple-element.8), channel_id=1, source_target_pairs={{0,8},{1,9}} | collective-permute-start | bytes 786440 | tf_op jit(solution)/shard_map/ppermute | solution.py:274
  8.7 1.1 %collective-permute-done = f32[256,256]{1,0:T(8,128)S(1)} collective-permute-done((f32[256,256]{1,0:T(8,128)S(1)}, f32[256,256]{1,0:T(8,128)S(1)}, u32[]{:S(2)}, u32[]{:S(2)}) %collective-permute-start) | collective-permute-done | bytes 262176 | tf_op jit(solution)/shard_map/ppermute | solution.py:274
  9.9 3.1 %collective-permute-start.1 = (f32[256,256]{1,0:T(8,128)S(1)}, f32[256,256]{1,0:T(8,128)S(1)}, u32[]{:S(2)}, u32[]{:S(2)}) collective-permute-start(f32[256,256]{1,0:T(8,128)S(1)} %broadcast_select_fusion), channel_id=1, source_target_pairs={{0,4},{1,5},{8,24},{9,25}} | collective-permute-start | bytes 786440 | tf_op jit(solution)/shard_map/ppermute | solution.py:283
  13.0 4.2 %collective-permute-done.1 = f32[256,256]{1,0:T(8,128)S(1)} collective-permute-done((f32[256,256]{1,0:T(8,128)S(1)}, f32[256,256]{1,0:T(8,128)S(1)}, u32[]{:S(2)}, u32[]{:S(2)}) %collective-permute-start.1) | collective-permute-done | bytes 262176 | tf_op jit(solution)/shard_map/ppermute | solution.py:283
  17.2 1.3 %collective-permute-start.2 = (f32[256,256]{1,0:T(8,128)S(1)}, f32[256,256]{1,0:T(8,128)S(1)}, u32[]{:S(2)}, u32[]{:S(2)}) collective-permute-start(f32[256,256]{1,0:T(8,128)S(1)} %broadcast_select_fusion.1), channel_id=1, source_target_pairs={{0,2},{1,3},{4,6},{5,7},{8,12},{9,13},{24,28},{25,29}} | collective-permute-start | bytes 786440 | tf_op jit(solution)/shard_map/ppermute | solution.py:283
  18.6 4.8 %collective-permute-done.2 = f32[256,256]{1,0:T(8,128)S(1)} collective-permute-done((f32[256,256]{1,0:T(8,128)S(1)}, f32[256,256]{1,0:T(8,128)S(1)}, u32[]{:S(2)}, u32[]{:S(2)}) %collective-permute-start.2) | collective-permute-done | bytes 262176 | tf_op jit(solution)/shard_map/ppermute | solution.py:283
  23.4 0.0 copy-start.1
  23.4 1.6 %collective-permute-start.3 = (f32[256,256]{1,0:T(8,128)S(1)}, f32[256,256]{1,0:T(8,128)S(1)}, u32[]{:S(2)}, u32[]{:S(2)}) collective-permute-start(f32[256,256]{1,0:T(8,128)S(1)} %broadcast_select_fusion.2), channel_id=1, source_target_pairs={{0,16},{1,17},{2,18},{3,19},{4,20},{5,21},{6,22},{7,23},{8,10},{9,... | collective-permute-start | bytes 786440 | tf_op jit(solution)/shard_map/ppermute | solution.py:283
  25.1 3.6 %collective-permute-done.3 = f32[256,256]{1,0:T(8,128)S(1)} collective-permute-done((f32[256,256]{1,0:T(8,128)S(1)}, f32[256,256]{1,0:T(8,128)S(1)}, u32[]{:S(2)}, u32[]{:S(2)}) %collective-permute-start.3) | collective-permute-done | bytes 262176 | tf_op jit(solution)/shard_map/ppermute | solution.py:283
  28.7 1.2 %collective-permute-start.4 = (f32[256,256]{1,0:T(8,128)S(1)}, f32[256,256]{1,0:T(8,128)S(1)}, u32[]{:S(2)}, u32[]{:S(2)}) collective-permute-start(f32[256,256]{1,0:T(8,128)S(1)} %broadcast_select_fusion.3.own), channel_id=1, source_target_pairs={{0,1},{1,0},{2,3},{3,2},{4,5},{5,4},{6,7},{7,6},{8,9},{9,8},{10,11... | collective-permute-start | bytes 786440 | tf_op jit(solution)/shard_map/ppermute | solution.py:330
  30.0 0.0 collective-permute-start.5
  30.0 5.2 %collective-permute-done.4.other = f32[256,256]{1,0:T(8,128)S(1)} collective-permute-done((f32[256,256]{1,0:T(8,128)S(1)}, f32[256,256]{1,0:T(8,128)S(1)}, u32[]{:S(2)}, u32[]{:S(2)}) %collective-permute-start.4) | collective-permute-done | bytes 262176 | tf_op jit(solution)/shard_map/ppermute | solution.py:330
  35.2 0.0 collective-permute-start.6
  35.2 0.0 collective-permute-done.5.own_swapped
  35.2 1.5 %collective-permute-done.6.other_swapped = f32[256,256]{1,0:T(8,128)S(1)} collective-permute-done((f32[256,256]{1,0:T(8,128)S(1)}, f32[256,256]{1,0:T(8,128)S(1)}, u32[]{:S(2)}, u32[]{:S(2)}) %collective-permute-start.6) | collective-permute-done | bytes 262176 | tf_op jit(solution)/shard_map/ppermute | solution.py:332
  36.7 0.0 copy-done.1
  36.7 20.3 %update.1 = (f32[256,512]{1,0:T(8,128)}, f32[256,256]{1,0:T(8,128)}, f32[256,128]{1,0:T(8,128)S(1)}) custom-call(s32[3]{0:T(128)S(1)} %pad_add_fusion.flags, f32[256,512]{1,0:T(8,128)S(1)} %bitcast.12, f32[256,256]{1,0:T(8,128)S(1)} %bitcast.14, f32[256,256]{1,0:T(8,128)S(1)} %broadcast_select_fusion.3.own, f32[256,256]{1,0:T(8,128)S(1)} %collective-permute-done.4.other, ...), custom_call_target="tpu_custom_call" | custom-call | flops 10000000000 | bytes 2097152 | tf_op jit(solution)/shard_map/update/pallas_call | solution.py:333
  57.0 15.2 %all_to_all.9 = f32[32,8,128]{2,1,0:T(8,128)S(1)} all-to-all(f32[32,8,128]{2,1,0:T(8,128)S(1)} %bitcast.15), channel_id=1, replica_groups=mesh['row'=4,'col'=8] {'row','col'}, dimensions={0} | all-to-all | bytes 262144 | tf_op jit(solution)/shard_map/all_to_all | solution.py:345
  72.3 0.6 sqrt_bitcast_fusion
  (7 shorter events, 0.2 us)
Async XLA Ops:
  0.7 1.0 %copy-start = (f32[1,256,512]{2,1,0:T(8,128)S(1)}, f32[1,256,512]{2,1,0:T(8,128)}, u32[]{:S(2)}) copy-start(f32[1,256,512]{2,1,0:T(8,128)} %param.2) | copy-start | bytes 1572868
  1.8 2.8 %copy-start.2 = (f32[1,256,256]{2,1,0:T(8,128)S(1)}, f32[1,256,256]{2,1,0:T(8,128)}, u32[]{:S(2)}) copy-start(f32[1,256,256]{2,1,0:T(8,128)} %param.3) | copy-start | bytes 786436
  6.3 3.5 %collective-permute-start = (f32[256,256]{1,0:T(8,128)S(1)}, f32[256,256]{1,0:T(8,128)S(1)}, u32[]{:S(2)}, u32[]{:S(2)}) collective-permute-start(f32[256,256]{1,0:T(8,128)S(1)} %get-tuple-element.8), channel_id=1, source_target_pairs={{0,8},{1,9}} | collective-permute-start | bytes 786440 | tf_op jit(solution)/shard_map/ppermute | solution.py:274
  9.9 7.3 %collective-permute-start.1 = (f32[256,256]{1,0:T(8,128)S(1)}, f32[256,256]{1,0:T(8,128)S(1)}, u32[]{:S(2)}, u32[]{:S(2)}) collective-permute-start(f32[256,256]{1,0:T(8,128)S(1)} %broadcast_select_fusion), channel_id=1, source_target_pairs={{0,4},{1,5},{8,24},{9,25}} | collective-permute-start | bytes 786440 | tf_op jit(solution)/shard_map/ppermute | solution.py:283
  17.2 6.1 %collective-permute-start.2 = (f32[256,256]{1,0:T(8,128)S(1)}, f32[256,256]{1,0:T(8,128)S(1)}, u32[]{:S(2)}, u32[]{:S(2)}) collective-permute-start(f32[256,256]{1,0:T(8,128)S(1)} %broadcast_select_fusion.1), channel_id=1, source_target_pairs={{0,2},{1,3},{4,6},{5,7},{8,12},{9,13},{24,28},{25,29}} | collective-permute-start | bytes 786440 | tf_op jit(solution)/shard_map/ppermute | solution.py:283
  23.4 13.3 %copy-start.1 = (f32[1,256,512]{2,1,0:T(8,128)S(1)}, f32[1,256,512]{2,1,0:T(8,128)}, u32[]{:S(2)}) copy-start(f32[1,256,512]{2,1,0:T(8,128)} %param.2) | copy-start | bytes 1572868
  23.4 5.3 %collective-permute-start.3 = (f32[256,256]{1,0:T(8,128)S(1)}, f32[256,256]{1,0:T(8,128)S(1)}, u32[]{:S(2)}, u32[]{:S(2)}) collective-permute-start(f32[256,256]{1,0:T(8,128)S(1)} %broadcast_select_fusion.2), channel_id=1, source_target_pairs={{0,16},{1,17},{2,18},{3,19},{4,20},{5,21},{6,22},{7,23},{8,10},{9,... | collective-permute-start | bytes 786440 | tf_op jit(solution)/shard_map/ppermute | solution.py:283
  28.7 6.4 %collective-permute-start.4 = (f32[256,256]{1,0:T(8,128)S(1)}, f32[256,256]{1,0:T(8,128)S(1)}, u32[]{:S(2)}, u32[]{:S(2)}) collective-permute-start(f32[256,256]{1,0:T(8,128)S(1)} %broadcast_select_fusion.3.own), channel_id=1, source_target_pairs={{0,1},{1,0},{2,3},{3,2},{4,5},{5,4},{6,7},{7,6},{8,9},{9,8},{10,11... | collective-permute-start | bytes 786440 | tf_op jit(solution)/shard_map/ppermute | solution.py:330
  30.0 5.2 %collective-permute-start.5 = (f32[256,256]{1,0:T(8,128)S(1)}, f32[256,256]{1,0:T(8,128)S(1)}, u32[]{:S(2)}, u32[]{:S(2)}) collective-permute-start(f32[256,256]{1,0:T(8,128)S(1)} %broadcast_select_fusion.3.own), channel_id=1, source_target_pairs={{0,8},{1,9},{2,10},{3,11},{4,12},{5,13},{6,14},{7,15},{8,0},{9,1},... | collective-permute-start | bytes 786440 | tf_op jit(solution)/shard_map/ppermute | solution.py:331
  35.2 1.5 %collective-permute-start.6 = (f32[256,256]{1,0:T(8,128)S(1)}, f32[256,256]{1,0:T(8,128)S(1)}, u32[]{:S(2)}, u32[]{:S(2)}) collective-permute-start(f32[256,256]{1,0:T(8,128)S(1)} %collective-permute-done.4.other), channel_id=1, source_target_pairs={{0,8},{1,9},{2,10},{3,11},{4,12},{5,13},{6,14},{7,15},{8,0},{9,1},... | collective-permute-start | bytes 786440 | tf_op jit(solution)/shard_map/ppermute | solution.py:332

commit v3 on v2

--- a/solution.py
+++ b/solution.py
@@ -9,6 +9,7 @@
 N = 128
 H = N // 2
 NB = H // T
+SMALL = 32
 AXES = ("row", "col")
 F32 = jnp.float32
 HI = lax.Precision.HIGHEST
@@ -43,7 +44,9 @@
         tile = jnp.where(sub <= j, rows[j], tile)
     return jnp.where(col <= sub + k, tile, 0.0)
 
-def chol_leaf(mat, sc, sl, sr):
+def chol_leaf(mat, sc, sl, sr, fill=()):
+    fill = list(fill)
+    rate = -(-len(fill) // NB)
     col, sub, base = half_masks()
     mat = list(mat)
     out = []
@@ -63,6 +66,8 @@
         if b < NB - 1:
             own = [pick(mat[b + 1], base, k + T + j) for j in range(T)]
         acc = {t: jnp.where(inside, 0.0, mat[t]) for t in below}
+        for task in fill[b * rate : (b + 1) * rate]:
+            task()
         for j in range(T):
             scale = lax.rsqrt(a[j, j])
             low = {i: a[i, j] * scale for i in range(j + 1, T)}
@@ -87,17 +92,20 @@
     return out
 
 def tri_leaf(mats, scs, srs):
-    col, sub, base = half_masks()
-    mats = [list(m) for m in mats]
+    lane = lax.broadcasted_iota(jnp.int32, (T, N), 1)
+    sub = lax.broadcasted_iota(jnp.int32, (T, N), 0)
+    col = lane % SMALL
+    base = lane - col
+    count = SMALL // T
     outs = [[] for _ in mats]
     picks = []
     for mat, sc in zip(mats, scs):
-        picks.append([{t: [pick(mat[t], base, b * T + j) for j in range(T)] for t in range(b, NB)} for b in range(NB)])
-        for b in range(NB):
+        picks.append([{t: [pick(mat[t], base, b * T + j) for j in range(T)] for t in range(b, count)} for b in range(count)])
+        for b in range(count):
             for j in range(T):
                 sc[b, j * T : (j + 1) * T, :] = picks[-1][b][b][j]
     mats = [[jnp.zeros((T, N), F32) for _ in m] for m in mats]
-    for b in range(NB):
+    for b in range(count):
         k = b * T
         inside = (col >= k) & (col < k + T)
         unit = (col == sub + k).astype(F32)
@@ -110,7 +118,7 @@
                 for i in range(j + 1, T):
                     r[i] = r[i] - row_bcast(cs, j * T + i) * r[j]
             outs[q].append(assemble(r, k, col, sub))
-            for t in range(b + 1, NB):
+            for t in range(b + 1, count):
                 for j in range(T):
                     mat[t] = mat[t] - picks[q][b][t][j] * r[j]
     return outs
@@ -120,75 +128,101 @@
     return jnp.concatenate([jnp.where(lane < H, x, 0.0), jnp.where(lane < H, 0.0, x)], axis=0)
 
 def pack(first, second):
-    lane = lax.broadcasted_iota(jnp.int32, (first.shape[0], N), 1)
-    out = []
-    for c in range(0, first.shape[1], N):
-        x, y = first[:, c : c + N], second[:, c : c + N]
-        out.append(jnp.where(lane < H, x, pltpu.roll(y, H, 1)))
-        out.append(jnp.where(lane < H, pltpu.roll(x, H, 1), y))
-    return out
+    lane = lax.broadcasted_iota(jnp.int32, first.shape, 1)
+    return (
+        jnp.where(lane < H, first, pltpu.roll(second, H, 1)),
+        jnp.where(lane < H, pltpu.roll(first, H, 1), second),
+    )
 
 def tiles_of(ref, r0, c0):
     return [ref[r0 + t * T : r0 + (t + 1) * T, c0 : c0 + N] for t in range(NB)]
 
-def chol_inverse_pair(gram, inv, tmp, sc, sl, sr):
+def chol_inverse_pair(gram, inv, tmp, parts, sc, sl, sr, fills):
     n = gram.shape[0]
     nb = n // H
-    low = {}
+    rows = lambda e: slice(e * H, (e + 1) * H)
+    cols = lambda e: slice(e * N, (e + 1) * N)
+    span = lambda e, f: slice(e * N, f * N)
+    pairs = lambda e, f: [(i, min(i + 2, f)) for i in range(e, f, 2)]
+
+    def solve(d, at):
+        tmp[at, cols(d)] = mm_nt(gram[at, cols(d)], split_halves(inv[rows(d), cols(d)]))
+
+    def shrink(d, e, f, at):
+        weights = jnp.concatenate([split_halves(tmp[rows(i), cols(d)]) for i in range(e, f)], axis=0)
+        gram[at, span(e, f)] = gram[at, span(e, f)] - mm_nt(tmp[at, cols(d)], weights)
+
+    def gather(d, e, f, c, b):
+        weights = jnp.concatenate(
+            [
+                jnp.concatenate([split_halves(inv[rows(i), cols(k)]) for k in range(c, b)], axis=1)
+                for i in range(e, f)
+            ],
+            axis=0,
+        )
+        part = mm(tmp[rows(d), span(e, f)], weights)
+        parts[:, span(c, b)] = part if e == 0 else parts[:, span(c, b)] + part
+
+    def finish(d, c, b):
+        weights = jnp.concatenate([split_halves(parts[:, cols(k)]) for k in range(c, b)], axis=1)
+        inv[rows(d), span(c, b)] = -mm(inv[rows(d), cols(d)], weights)
+
+    inv[...] = jnp.zeros(inv.shape, F32)
+    pending = []
     for d in range(nb):
-        at = slice(d * H, (d + 1) * H)
-        for t, tile in enumerate(chol_leaf(tiles_of(gram, d * H, d * N), sc, sl, sr)):
-            inv[d * H + t * T : d * H + (t + 1) * T, d * N : (d + 1) * N] = tile
-        w = inv[at, d * N : (d + 1) * N]
+        tasks = pending + [lambda e=e, f=f, c=c, b=b: gather(d, e, f, c, b) for e, f in pairs(0, d) for c, b in pairs(0, d)]
+        tasks += fills.get(d, [])
+        for t, tile in enumerate(chol_leaf(tiles_of(gram, d * H, d * N), sc, sl, sr, tasks)):
+            inv[d * H + t * T : d * H + (t + 1) * T, cols(d)] = tile
+        pending = []
         if d < nb - 1:
-            rest = slice((d + 1) * H, n)
-            tmp[rest, d * N : (d + 1) * N] = mm_nt(gram[rest, d * N : (d + 1) * N], split_halves(w))
-            for e in range(d + 1, nb):
-                rows = slice(e * H, n)
-                cols = slice(e * N, (e + 1) * N)
-                gram[rows, cols] = gram[rows, cols] - mm_nt(
-                    tmp[rows, d * N : (d + 1) * N], split_halves(tmp[e * H : (e + 1) * H, d * N : (d + 1) * N])
-                )
-        for c in range(d):
-            cols = slice(c * N, (c + 1) * N)
-            part = None
-            for e in range(c, d):
-                term = mm(tmp[at, e * N : (e + 1) * N], split_halves(inv[e * H : (e + 1) * H, cols]))
-                part = term if part is None else part + term
-            inv[at, cols] = -mm(w, split_halves(part))
+            solve(d, rows(d + 1))
+            shrink(d, d + 1, d + 2, rows(d + 1))
+            if d + 2 < nb:
+                later = slice((d + 2) * H, n)
+                pending.append(lambda d=d, at=later: solve(d, at))
+                pending.append(lambda d=d, at=later: shrink(d, d + 1, d + 3, at))
+            for e, f in pairs(d + 3, nb):
+                pending.append(lambda d=d, e=e, f=f: shrink(d, e, f, slice(e * H, n)))
+            pending += [lambda d=d, c=c, b=b: finish(d, c, b) for c, b in pairs(0, d)]
+        else:
+            for c, b in pairs(0, d):
+                finish(d, c, b)
 
 def unpack(inv, first, second):
     n = inv.shape[0]
-    lane = lax.broadcasted_iota(jnp.int32, (n, N), 1)
-    row = lax.broadcasted_iota(jnp.int32, (n, N), 0)
     for c in range(0, n, N):
-        x, y = inv[:, 2 * c : 2 * c + N], inv[:, 2 * c + N : 2 * c + 2 * N]
-        x = jnp.where(row >= c, x, 0.0)
-        y = jnp.where(row >= c + H, y, 0.0)
-        first[:, c : c + N] = jnp.where(lane < H, x, pltpu.roll(y, H, 1))
-        second[:, c : c + N] = jnp.where(lane < H, pltpu.roll(x, H, 1), y)
+        first[:, c : c + N], second[:, c : c + N] = pack(inv[:, 2 * c : 2 * c + N], inv[:, 2 * c + N : 2 * c + 2 * N])
 
 def tri_inverse(block, inverse, scs, srs):
     n = block.shape[0]
     lane = lax.broadcasted_iota(jnp.int32, (T, N), 1)
     mats = []
     for c in range(0, n, N):
-        mats.append([
-            jnp.where(lane < H, block[c + t * T : c + (t + 1) * T, c : c + N], block[c + H + t * T : c + H + (t + 1) * T, c : c + N])
-            for t in range(NB)
-        ])
+        tiles = []
+        for t in range(SMALL // T):
+            tile = block[c + t * T : c + (t + 1) * T, c : c + N]
+            for i in range(SMALL, N, SMALL):
+                tile = jnp.where(lane < i, tile, block[c + i + t * T : c + i + (t + 1) * T, c : c + N])
+            tiles.append(tile)
+        mats.append(tiles)
     outs = tri_leaf(mats, scs, srs)
+    row = lax.broadcasted_iota(jnp.int32, (N, N), 0)
+    col = lax.broadcasted_iota(jnp.int32, (N, N), 1)
     for c, out in zip(range(0, n, N), outs):
-        for t, tile in enumerate(out):
-            inverse[c + t * T : c + (t + 1) * T, c : c + N] = jnp.where(lane < H, tile, 0.0)
-            inverse[c + H + t * T : c + H + (t + 1) * T, c : c + N] = jnp.where(lane < H, 0.0, tile)
-    big = lax.broadcasted_iota(jnp.int32, (H, N), 1)
+        for i in range(0, N, SMALL):
+            for t, tile in enumerate(out):
+                inverse[c + i + t * T : c + i + (t + 1) * T, c : c + N] = jnp.where(
+                    (lane >= i) & (lane < i + SMALL), tile, 0.0
+                )
     for c in range(0, n, N):
-        diag = inverse[c : c + N, c : c + N]
-        corner = jnp.where(big < H, block[c + H : c + N, c : c + N], 0.0)
-        t1 = mm(corner, diag)
-        t2 = mm(diag[H:, :], jnp.concatenate([jnp.zeros((H, N), F32), t1], axis=0))
-        inverse[c + H : c + N, c : c + N] = diag[H:, :] - t2
+        value = inverse[c : c + N, c : c + N]
+        size = SMALL
+        while size < N:
+            corner = (row // size == col // size + 1) & (row // size % 2 == 1)
+            value = value - mm(value, mm(jnp.where(corner, block[c : c + N, c : c + N], 0.0), value))
+            size *= 2
+        inverse[c : c + N, c : c + N] = value
 
 
 def inverse_kernel(flags, factor, inverse, scs, srs):
@@ -214,54 +248,70 @@
         out[:, half:] = rhs[:, width + low : width + low + half]
 
 
-def panel_step(columns, current, g, new_columns, inv_l, inv_c, gram, inv, tmp, sc, sl, sr):
-    width = g.shape[0]
-    eye = (
-        lax.broadcasted_iota(jnp.int32, (width, width), 0)
-        == lax.broadcasted_iota(jnp.int32, (width, width), 1)
-    ).astype(F32)
-    x = g[...]
-    for c, part in enumerate(pack(eye + mm_nt(x, x), eye + mm_tn(x, x))):
-        gram[:, c * N : (c + 1) * N] = part
-    cols = columns[...]
-    v = current[...]
-    new_columns[...] = cols + mm_nt(v, x)
-    current[...] = v - mm(cols, x)
-    chol_inverse_pair(gram, inv, tmp, sc, sl, sr)
-    unpack(inv, inv_l, inv_c)
-    new_columns[...] = mm_nt(new_columns[...], inv_l[...])
-    current[...] = mm_nt(current[...], inv_c[...])
+def gram_rows(g, gram, low, high, width):
+    row = lax.broadcasted_iota(jnp.int32, (high - low, width), 0) + low
+    eye = (row == lax.broadcasted_iota(jnp.int32, (high - low, width), 1)).astype(F32)
+    first = eye + mm_nt(g[low:high, :], g[:width, :])
+    left = g[:, :N] if high <= N else g[...]
+    second = eye + mm_tn(left, g[:, :width])[low:high, :]
+    for c in range(0, width, N):
+        gram[low:high, 2 * c : 2 * c + N], gram[low:high, 2 * c + N : 2 * c + 2 * N] = pack(
+            first[:, c : c + N], second[:, c : c + N]
+        )
 
 
 def update_kernel(
     flags, factor, update, own, other, own_swapped, other_swapped,
-    new_factor, current, copies, g, x, inv_l, inv_c, *rest,
+    new_factor, new_update, copies, g, x, y, mixed, current, inv_l, inv_c, gram, inv, tmp, parts, sc, sl, sr,
 ):
     width = g.shape[0]
     half = width // 2
+    panels = factor.shape[1] // width
     south = flags[1] == 1
     odd = flags[2] == 1
-
-    def halves(low, swap):
+    part = lambda p: slice(p * width, (p + 1) * width)
+
+    def halves(out, low, swap):
         at = slice(low, low + half)
         here = jnp.where(odd != swap, other[:, at], own[:, at])
         there = jnp.where(odd != swap, other_swapped[:, at], own_swapped[:, at])
-        return jnp.where(south, there, here), jnp.where(south, here, there)
-
-    g[:, :half], g[:, half:] = halves(0, False)
-    y = jnp.concatenate(halves(half, True), axis=1)
-    x[...] = jnp.concatenate(halves(0, True), axis=1) - mm(y, g[...])
-    current[...] = update[...]
-    panel_step(factor.at[:, :width], current, g, new_factor.at[:, :width], inv_l, inv_c, *rest)
-    x[...] = mm_nt(x[...], inv_c[...])
-    panel_step(factor.at[:, width:], current, x, new_factor.at[:, width:], inv_l, inv_c, *rest)
+        out[:, :half] = jnp.where(south, there, here)
+        out[:, half:] = jnp.where(south, here, there)
+
+    def mix(p):
+        v = update if p == 0 else new_update
+        mixed[...] = factor[:, part(p)] + mm_nt(v[...], g[...])
+
+    def lower(p):
+        v = update if p == 0 else new_update
+        current[...] = v[...] - mm(factor[:, part(p)], g[...])
+
+    def carry():
+        x[...] = x[...] - mm(y[...], g[...])
+
+    def columns(p):
+        new_factor[:, part(p)] = mm_nt(mixed[...], inv_l[...])
+
+    def updates():
+        new_update[...] = mm_nt(current[...], inv_c[...])
+
+    halves(g, 0, False)
+    halves(y, half, True)
+    halves(x, 0, True)
+    held = []
+    for p in range(panels):
+        gram_rows(g, gram, 0, H, N)
+        rest = [lambda: gram_rows(g, gram, H, width, width)]
+        tasks = {0: rest + held, 1: [lambda: mix(p), lambda: lower(p)], 2: [carry] if p < panels - 1 else []}
+        chol_inverse_pair(gram, inv, tmp, parts, sc, sl, sr, tasks)
+        unpack(inv, inv_l, inv_c)
+        held = [lambda p=p: columns(p), updates]
+        if p < panels - 1:
+            g[...] = mm_nt(x[...], inv_c[...])
+    for task in held:
+        task()
     squares = jnp.sum(new_factor[...] * new_factor[...], axis=0, keepdims=True)
-    sub = lax.broadcasted_iota(jnp.int32, (T, N), 0)
-    tile = jnp.zeros((T, N), F32)
-    for c in range(squares.shape[1] // N):
-        tile = jnp.where(sub == c, squares[:, c * N : (c + 1) * N], tile)
-    for d in range(copies.shape[0] // T):
-        copies[d * T : (d + 1) * T, :] = tile
+    copies[...] = jnp.broadcast_to(squares, copies.shape)
 
 
 def masks_of(rows, cols):
@@ -332,18 +382,20 @@
     other_swapped = lax.ppermute(other, AXES, partner)
     new_factor, new_update, copies = pl.pallas_call(
         update_kernel,
-        out_shape=(shape(tile, wide), shape(tile, width), shape(total * T, N)),
+        out_shape=(shape(tile, wide), shape(tile, width), shape(total, wide)),
         in_specs=[smem] + [vmem] * 6,
         out_specs=(vmem,) * 3,
-        scratch_shapes=[work(width, width)] * 4
+        scratch_shapes=[work(width, width)] * 3
+        + [work(tile, width)] * 2
+        + [work(width, width)] * 2
         + [work(width, 2 * width)] * 3
-        + [work(2, T * T, N), work(2, T * T, N), work(2, T, N)],
+        + [work(H, 2 * width), work(2, T * T, N), work(2, T * T, N), work(2, T, N)],
         compiler_params=limit,
         cost_estimate=pl.CostEstimate(flops=10 ** 10, bytes_accessed=2 ** 21, transcendentals=0),
         name="update",
     )(flags, flat_factor, flat_update, own, other, own_swapped, other_swapped)
     gathered = lax.all_to_all(copies, AXES, 0, 0, tiled=True)
-    squares = jnp.sum(gathered.reshape(total, T, N), axis=0)[: wide // N].reshape(wide)
+    squares = jnp.sum(gathered, axis=0)
     column_scale = jnp.sqrt(squares / (tile * total) + 1e-06)
     return (new_factor.reshape(factor.shape), new_update.reshape(update.shape), column_scale)
 

time: 73.2 us -> 70.5 us (0.963)
  Pallas kernels: 24.8 us -> 22.6 us
    pallas_call x1, Pallas kernels: 20.3 us -> 18.6 us  [on_device(): pl.pallas_call(update_kernel, out_shape=(shape(tile, wide), shape(tile, w...]
where the time goes in v3:
time: 70.5 us; the launch traced here: 70.3 us
  Pallas kernels  22.6 us (32%)
  waiting for transfers between devices  20.4 us (29%)
  blocking collectives  14.7 us (21%)
  starting transfers between devices  9.72 us (14%)
  local copies, waits for them, and re-layouts  1.12 us (2%)
  other arithmetic  0.87 us (1%)
  between operations  0.83 us (1%)
    pallas_call x1, Pallas kernels, on_device(): pl.pallas_call(update_kernel, out_shape=(shape(tile, wide), shape(tile, w...  18.6 us
    all_to_all x1, blocking collectives, on_device(): gathered = lax.all_to_all(copies, AXES, 0, 0, tiled=True)  14.7 us
    ppermute x3, waiting for transfers between devices, spread(): came = lax.ppermute(part, AXES, pairs)  12.5 us
    ppermute x3, starting transfers between devices, spread(): came = lax.ppermute(part, AXES, pairs)  6.07 us
    ppermute x1, waiting for transfers between devices, on_device(): other = lax.ppermute(own, AXES, [(d, d ^ 1) for d in range(total)])  5.19 us
    ppermute x1, starting transfers between devices, spread(): sent = lax.ppermute(right, AXES, [(d, d | core) for d in roots])  2.41 us
    pallas_call x1, Pallas kernels, on_device(): pl.pallas_call(inverse_kernel, out_shape=shape(width, width), in_specs=[s...  2.31 us
    pallas_call x1, Pallas kernels, on_device(): pl.pallas_call(solve_kernel, out_shape=(shape(width, width),) * 2, in_spe...  1.73 us
  transfers between devices with their start and end apart: 7, of which 6 were waited for; matrix products, arithmetic and copies ran while one was open for 0% of the time, Pallas kernels for 0%

profile of v3, /device:TPU:0, one launch (start us, length us, event | category | flops | bytes accessed | tf_op | source)
XLA Modules:
  0.0 70.3 jit_solution(7162294865477885109)
XLA Ops:
  0.6 0.1 pad_add_fusion.flags
  0.7 1.0 %copy-done = f32[1,256,512]{2,1,0:T(8,128)S(1)} copy-done((f32[1,256,512]{2,1,0:T(8,128)S(1)}, f32[1,256,512]{2,1,0:T(8,128)}, u32[]{:S(2)}) %copy-start) | copy-done | bytes 524312
  1.8 2.3 %inverse.1 = f32[256,256]{1,0:T(8,128)S(1)} custom-call(s32[3]{0:T(128)S(1)} %pad_add_fusion.flags, f32[256,512]{1,0:T(8,128)S(1)} %bitcast.8), custom_call_target="tpu_custom_call" | custom-call | tf_op jit(solution)/shard_map/inverse/pallas_call | solution.py:360
  4.1 1.7 %solve.1 = (f32[256,256]{1,0:T(8,128)S(1)}, f32[256,256]{1,0:T(8,128)S(1)}) custom-call(s32[3]{0:T(128)S(1)} %pad_add_fusion.flags, f32[256,512]{1,0:T(8,128)S(1)} %bitcast.9, f32[256,256]{1,0:T(8,128)S(1)} %bitcast.11, f32[256,256]{1,0:T(8,128)S(1)} %inverse.1), custom_call_target="tpu_custom_call" | custom-call | tf_op jit(solution)/shard_map/solve/pallas_call | solution.py:369
  5.8 2.4 %collective-permute-start = (f32[256,256]{1,0:T(8,128)S(1)}, f32[256,256]{1,0:T(8,128)S(1)}, u32[]{:S(2)}, u32[]{:S(2)}) collective-permute-start(f32[256,256]{1,0:T(8,128)S(1)} %get-tuple-element.8), channel_id=1, source_target_pairs={{0,8},{1,9}} | collective-permute-start | bytes 786440 | tf_op jit(solution)/shard_map/ppermute | solution.py:324
  8.2 1.1 %collective-permute-done = f32[256,256]{1,0:T(8,128)S(1)} collective-permute-done((f32[256,256]{1,0:T(8,128)S(1)}, f32[256,256]{1,0:T(8,128)S(1)}, u32[]{:S(2)}, u32[]{:S(2)}) %collective-permute-start) | collective-permute-done | bytes 262176 | tf_op jit(solution)/shard_map/ppermute | solution.py:324
  9.4 3.1 %collective-permute-start.1 = (f32[256,256]{1,0:T(8,128)S(1)}, f32[256,256]{1,0:T(8,128)S(1)}, u32[]{:S(2)}, u32[]{:S(2)}) collective-permute-start(f32[256,256]{1,0:T(8,128)S(1)} %broadcast_select_fusion), channel_id=1, source_target_pairs={{0,4},{1,5},{8,24},{9,25}} | collective-permute-start | bytes 786440 | tf_op jit(solution)/shard_map/ppermute | solution.py:333
  12.6 4.2 %collective-permute-done.1 = f32[256,256]{1,0:T(8,128)S(1)} collective-permute-done((f32[256,256]{1,0:T(8,128)S(1)}, f32[256,256]{1,0:T(8,128)S(1)}, u32[]{:S(2)}, u32[]{:S(2)}) %collective-permute-start.1) | collective-permute-done | bytes 262176 | tf_op jit(solution)/shard_map/ppermute | solution.py:333
  16.8 1.3 %collective-permute-start.2 = (f32[256,256]{1,0:T(8,128)S(1)}, f32[256,256]{1,0:T(8,128)S(1)}, u32[]{:S(2)}, u32[]{:S(2)}) collective-permute-start(f32[256,256]{1,0:T(8,128)S(1)} %broadcast_select_fusion.1), channel_id=1, source_target_pairs={{0,2},{1,3},{4,6},{5,7},{8,12},{9,13},{24,28},{25,29}} | collective-permute-start | bytes 786440 | tf_op jit(solution)/shard_map/ppermute | solution.py:333
  18.1 4.8 %collective-permute-done.2 = f32[256,256]{1,0:T(8,128)S(1)} collective-permute-done((f32[256,256]{1,0:T(8,128)S(1)}, f32[256,256]{1,0:T(8,128)S(1)}, u32[]{:S(2)}, u32[]{:S(2)}) %collective-permute-start.2) | collective-permute-done | bytes 262176 | tf_op jit(solution)/shard_map/ppermute | solution.py:333
  22.9 0.0 copy-start.1
  22.9 1.6 %collective-permute-start.3 = (f32[256,256]{1,0:T(8,128)S(1)}, f32[256,256]{1,0:T(8,128)S(1)}, u32[]{:S(2)}, u32[]{:S(2)}) collective-permute-start(f32[256,256]{1,0:T(8,128)S(1)} %broadcast_select_fusion.2), channel_id=1, source_target_pairs={{0,16},{1,17},{2,18},{3,19},{4,20},{5,21},{6,22},{7,23},{8,10},{9,... | collective-permute-start | bytes 786440 | tf_op jit(solution)/shard_map/ppermute | solution.py:333
  24.6 3.6 %collective-permute-done.3 = f32[256,256]{1,0:T(8,128)S(1)} collective-permute-done((f32[256,256]{1,0:T(8,128)S(1)}, f32[256,256]{1,0:T(8,128)S(1)}, u32[]{:S(2)}, u32[]{:S(2)}) %collective-permute-start.3) | collective-permute-done | bytes 262176 | tf_op jit(solution)/shard_map/ppermute | solution.py:333
  28.3 1.2 %collective-permute-start.4 = (f32[256,256]{1,0:T(8,128)S(1)}, f32[256,256]{1,0:T(8,128)S(1)}, u32[]{:S(2)}, u32[]{:S(2)}) collective-permute-start(f32[256,256]{1,0:T(8,128)S(1)} %broadcast_select_fusion.3.own), channel_id=1, source_target_pairs={{0,1},{1,0},{2,3},{3,2},{4,5},{5,4},{6,7},{7,6},{8,9},{9,8},{10,11... | collective-permute-start | bytes 786440 | tf_op jit(solution)/shard_map/ppermute | solution.py:380
  29.5 0.0 collective-permute-start.5
  29.5 5.2 %collective-permute-done.4.other = f32[256,256]{1,0:T(8,128)S(1)} collective-permute-done((f32[256,256]{1,0:T(8,128)S(1)}, f32[256,256]{1,0:T(8,128)S(1)}, u32[]{:S(2)}, u32[]{:S(2)}) %collective-permute-start.4) | collective-permute-done | bytes 262176 | tf_op jit(solution)/shard_map/ppermute | solution.py:380
  34.7 0.0 collective-permute-start.6
  34.7 0.0 collective-permute-done.5.own_swapped
  34.7 1.5 %collective-permute-done.6.other_swapped = f32[256,256]{1,0:T(8,128)S(1)} collective-permute-done((f32[256,256]{1,0:T(8,128)S(1)}, f32[256,256]{1,0:T(8,128)S(1)}, u32[]{:S(2)}, u32[]{:S(2)}) %collective-permute-start.6) | collective-permute-done | bytes 262176 | tf_op jit(solution)/shard_map/ppermute | solution.py:382
  36.2 18.6 %update.1 = (f32[256,512]{1,0:T(8,128)}, f32[256,256]{1,0:T(8,128)}, f32[32,512]{1,0:T(8,128)S(1)}) custom-call(s32[3]{0:T(128)S(1)} %pad_add_fusion.flags, f32[256,512]{1,0:T(8,128)S(1)} %bitcast.10, f32[256,256]{1,0:T(8,128)S(1)} %bitcast.12, f32[256,256]{1,0:T(8,128)S(1)} %broadcast_select_fusion.3.own, f32[256,256]{1,0:T(8,128)S(1)} %collective-permute-done.4.other, ...), custom_call_target="tpu_custom_call" | custom-call | flops 10000000000 | bytes 2097152 | tf_op jit(solution)/shard_map/update/pallas_call | solution.py:383
  54.8 0.1 copy.5
  54.9 14.7 %all_to_all.9 = f32[32,1,512]{2,1,0:T(1,128)S(1)} all-to-all(f32[32,1,512]{2,1,0:T(1,128)S(1)} %copy.5), channel_id=1, replica_groups=mesh['row'=4,'col'=8] {'row','col'}, dimensions={0} | all-to-all | bytes 131072 | tf_op jit(solution)/shard_map/all_to_all | solution.py:397
  69.6 0.1 reduce_sum.9
  69.7 0.6 add_sqrt_fusion
  (8 shorter events, 0.1 us)
Async XLA Ops:
  0.7 1.0 %copy-start = (f32[1,256,512]{2,1,0:T(8,128)S(1)}, f32[1,256,512]{2,1,0:T(8,128)}, u32[]{:S(2)}) copy-start(f32[1,256,512]{2,1,0:T(8,128)} %param.2) | copy-start | bytes 1572868
  1.8 2.3 %copy-start.2 = (f32[1,256,256]{2,1,0:T(8,128)S(1)}, f32[1,256,256]{2,1,0:T(8,128)}, u32[]{:S(2)}) copy-start(f32[1,256,256]{2,1,0:T(8,128)} %param.3) | copy-start | bytes 786436
  5.8 3.5 %collective-permute-start = (f32[256,256]{1,0:T(8,128)S(1)}, f32[256,256]{1,0:T(8,128)S(1)}, u32[]{:S(2)}, u32[]{:S(2)}) collective-permute-start(f32[256,256]{1,0:T(8,128)S(1)} %get-tuple-element.8), channel_id=1, source_target_pairs={{0,8},{1,9}} | collective-permute-start | bytes 786440 | tf_op jit(solution)/shard_map/ppermute | solution.py:324
  9.4 7.3 %collective-permute-start.1 = (f32[256,256]{1,0:T(8,128)S(1)}, f32[256,256]{1,0:T(8,128)S(1)}, u32[]{:S(2)}, u32[]{:S(2)}) collective-permute-start(f32[256,256]{1,0:T(8,128)S(1)} %broadcast_select_fusion), channel_id=1, source_target_pairs={{0,4},{1,5},{8,24},{9,25}} | collective-permute-start | bytes 786440 | tf_op jit(solution)/shard_map/ppermute | solution.py:333
  16.8 6.1 %collective-permute-start.2 = (f32[256,256]{1,0:T(8,128)S(1)}, f32[256,256]{1,0:T(8,128)S(1)}, u32[]{:S(2)}, u32[]{:S(2)}) collective-permute-start(f32[256,256]{1,0:T(8,128)S(1)} %broadcast_select_fusion.1), channel_id=1, source_target_pairs={{0,2},{1,3},{4,6},{5,7},{8,12},{9,13},{24,28},{25,29}} | collective-permute-start | bytes 786440 | tf_op jit(solution)/shard_map/ppermute | solution.py:333
  22.9 13.3 %copy-start.1 = (f32[1,256,512]{2,1,0:T(8,128)S(1)}, f32[1,256,512]{2,1,0:T(8,128)}, u32[]{:S(2)}) copy-start(f32[1,256,512]{2,1,0:T(8,128)} %param.2) | copy-start | bytes 1572868
  22.9 5.3 %collective-permute-start.3 = (f32[256,256]{1,0:T(8,128)S(1)}, f32[256,256]{1,0:T(8,128)S(1)}, u32[]{:S(2)}, u32[]{:S(2)}) collective-permute-start(f32[256,256]{1,0:T(8,128)S(1)} %broadcast_select_fusion.2), channel_id=1, source_target_pairs={{0,16},{1,17},{2,18},{3,19},{4,20},{5,21},{6,22},{7,23},{8,10},{9,... | collective-permute-start | bytes 786440 | tf_op jit(solution)/shard_map/ppermute | solution.py:333
  28.3 6.4 %collective-permute-start.4 = (f32[256,256]{1,0:T(8,128)S(1)}, f32[256,256]{1,0:T(8,128)S(1)}, u32[]{:S(2)}, u32[]{:S(2)}) collective-permute-start(f32[256,256]{1,0:T(8,128)S(1)} %broadcast_select_fusion.3.own), channel_id=1, source_target_pairs={{0,1},{1,0},{2,3},{3,2},{4,5},{5,4},{6,7},{7,6},{8,9},{9,8},{10,11... | collective-permute-start | bytes 786440 | tf_op jit(solution)/shard_map/ppermute | solution.py:380
  29.5 5.2 %collective-permute-start.5 = (f32[256,256]{1,0:T(8,128)S(1)}, f32[256,256]{1,0:T(8,128)S(1)}, u32[]{:S(2)}, u32[]{:S(2)}) collective-permute-start(f32[256,256]{1,0:T(8,128)S(1)} %broadcast_select_fusion.3.own), channel_id=1, source_target_pairs={{0,8},{1,9},{2,10},{3,11},{4,12},{5,13},{6,14},{7,15},{8,0},{9,1},... | collective-permute-start | bytes 786440 | tf_op jit(solution)/shard_map/ppermute | solution.py:381
  34.7 1.5 %collective-permute-start.6 = (f32[256,256]{1,0:T(8,128)S(1)}, f32[256,256]{1,0:T(8,128)S(1)}, u32[]{:S(2)}, u32[]{:S(2)}) collective-permute-start(f32[256,256]{1,0:T(8,128)S(1)} %collective-permute-done.4.other), channel_id=1, source_target_pairs={{0,8},{1,9},{2,10},{3,11},{4,12},{5,13},{6,14},{7,15},{8,0},{9,1},... | collective-permute-start | bytes 786440 | tf_op jit(solution)/shard_map/ppermute | solution.py:382

commit v4 on v3

--- a/solution.py
+++ b/solution.py
@@ -321,6 +321,7 @@
 
 def spread(left, right, my_index, core, steps, roots):
     turned = steps[-1:] + steps[:-1]
+    steps = steps[:1] + steps[-1:] + steps[1:-1]
     sent = lax.ppermute(right, AXES, [(d, d | core) for d in roots])
     part = jnp.where((my_index & core) != 0, sent, left)
     seen = [set(roots), {core | d for d in roots}]

time: 70.5 us -> 70.2 us (level)
  waiting for transfers between devices: 20.4 us -> 19.1 us
    ppermute x3, waiting for transfers between devices: 12.5 us -> 11.6 us  [spread(): came = lax.ppermute(part, AXES, pairs)]
where the time goes in v4:
time: 70.2 us; the launch traced here: 69.9 us
  Pallas kernels  22.6 us (32%)
  waiting for transfers between devices  19.1 us (27%)
  blocking collectives  15.3 us (22%)
  starting transfers between devices  10.1 us (14%)
  local copies, waits for them, and re-layouts  1.12 us (2%)
  other arithmetic  0.87 us (1%)
  between operations  0.83 us (1%)
    pallas_call x1, Pallas kernels, on_device(): pl.pallas_call(update_kernel, out_shape=(shape(tile, wide), shape(tile, w...  18.6 us
    all_to_all x1, blocking collectives, on_device(): gathered = lax.all_to_all(copies, AXES, 0, 0, tiled=True)  15.3 us
    ppermute x3, waiting for transfers between devices, spread(): came = lax.ppermute(part, AXES, pairs)  11.6 us
    ppermute x3, starting transfers between devices, spread(): came = lax.ppermute(part, AXES, pairs)  6.07 us
    ppermute x1, waiting for transfers between devices, on_device(): other = lax.ppermute(own, AXES, [(d, d ^ 1) for d in range(total)])  4.84 us
    ppermute x1, starting transfers between devices, spread(): sent = lax.ppermute(right, AXES, [(d, d | core) for d in roots])  2.41 us
    pallas_call x1, Pallas kernels, on_device(): pl.pallas_call(inverse_kernel, out_shape=shape(width, width), in_specs=[s...  2.31 us
    pallas_call x1, Pallas kernels, on_device(): pl.pallas_call(solve_kernel, out_shape=(shape(width, width),) * 2, in_spe...  1.73 us
  transfers between devices with their start and end apart: 7, of which 6 were waited for; matrix products, arithmetic and copies ran while one was open for 0% of the time, Pallas kernels for 0%

profile of v4, /device:TPU:0, one launch (start us, length us, event | category | flops | bytes accessed | tf_op | source)
XLA Modules:
  0.0 69.9 jit_solution(1363215333117992679)
XLA Ops:
  0.6 0.1 pad_add_fusion.flags
  0.7 1.0 %copy-done = f32[1,256,512]{2,1,0:T(8,128)S(1)} copy-done((f32[1,256,512]{2,1,0:T(8,128)S(1)}, f32[1,256,512]{2,1,0:T(8,128)}, u32[]{:S(2)}) %copy-start) | copy-done | bytes 524312
  1.8 2.3 %inverse.1 = f32[256,256]{1,0:T(8,128)S(1)} custom-call(s32[3]{0:T(128)S(1)} %pad_add_fusion.flags, f32[256,512]{1,0:T(8,128)S(1)} %bitcast.8), custom_call_target="tpu_custom_call" | custom-call | tf_op jit(solution)/shard_map/inverse/pallas_call | solution.py:361
  4.1 1.7 %solve.1 = (f32[256,256]{1,0:T(8,128)S(1)}, f32[256,256]{1,0:T(8,128)S(1)}) custom-call(s32[3]{0:T(128)S(1)} %pad_add_fusion.flags, f32[256,512]{1,0:T(8,128)S(1)} %bitcast.9, f32[256,256]{1,0:T(8,128)S(1)} %bitcast.11, f32[256,256]{1,0:T(8,128)S(1)} %inverse.1), custom_call_target="tpu_custom_call" | custom-call | tf_op jit(solution)/shard_map/solve/pallas_call | solution.py:370
  5.8 2.4 %collective-permute-start = (f32[256,256]{1,0:T(8,128)S(1)}, f32[256,256]{1,0:T(8,128)S(1)}, u32[]{:S(2)}, u32[]{:S(2)}) collective-permute-start(f32[256,256]{1,0:T(8,128)S(1)} %get-tuple-element.8), channel_id=1, source_target_pairs={{0,8},{1,9}} | collective-permute-start | bytes 786440 | tf_op jit(solution)/shard_map/ppermute | solution.py:325
  8.2 1.1 %collective-permute-done = f32[256,256]{1,0:T(8,128)S(1)} collective-permute-done((f32[256,256]{1,0:T(8,128)S(1)}, f32[256,256]{1,0:T(8,128)S(1)}, u32[]{:S(2)}, u32[]{:S(2)}) %collective-permute-start) | collective-permute-done | bytes 262176 | tf_op jit(solution)/shard_map/ppermute | solution.py:325
  9.4 3.1 %collective-permute-start.1 = (f32[256,256]{1,0:T(8,128)S(1)}, f32[256,256]{1,0:T(8,128)S(1)}, u32[]{:S(2)}, u32[]{:S(2)}) collective-permute-start(f32[256,256]{1,0:T(8,128)S(1)} %broadcast_select_fusion), channel_id=1, source_target_pairs={{0,4},{1,5},{8,24},{9,25}} | collective-permute-start | bytes 786440 | tf_op jit(solution)/shard_map/ppermute | solution.py:334
  12.6 4.2 %collective-permute-done.1 = f32[256,256]{1,0:T(8,128)S(1)} collective-permute-done((f32[256,256]{1,0:T(8,128)S(1)}, f32[256,256]{1,0:T(8,128)S(1)}, u32[]{:S(2)}, u32[]{:S(2)}) %collective-permute-start.1) | collective-permute-done | bytes 262176 | tf_op jit(solution)/shard_map/ppermute | solution.py:334
  16.8 1.3 %collective-permute-start.2 = (f32[256,256]{1,0:T(8,128)S(1)}, f32[256,256]{1,0:T(8,128)S(1)}, u32[]{:S(2)}, u32[]{:S(2)}) collective-permute-start(f32[256,256]{1,0:T(8,128)S(1)} %broadcast_select_fusion.1), channel_id=1, source_target_pairs={{0,16},{1,17},{4,20},{5,21},{8,12},{9,13},{24,28},{25,29}} | collective-permute-start | bytes 786440 | tf_op jit(solution)/shard_map/ppermute | solution.py:334
  18.1 3.8 %collective-permute-done.2 = f32[256,256]{1,0:T(8,128)S(1)} collective-permute-done((f32[256,256]{1,0:T(8,128)S(1)}, f32[256,256]{1,0:T(8,128)S(1)}, u32[]{:S(2)}, u32[]{:S(2)}) %collective-permute-start.2) | collective-permute-done | bytes 262176 | tf_op jit(solution)/shard_map/ppermute | solution.py:334
  22.0 0.0 copy-start.1
  22.0 1.6 %collective-permute-start.3 = (f32[256,256]{1,0:T(8,128)S(1)}, f32[256,256]{1,0:T(8,128)S(1)}, u32[]{:S(2)}, u32[]{:S(2)}) collective-permute-start(f32[256,256]{1,0:T(8,128)S(1)} %broadcast_select_fusion.2), channel_id=1, source_target_pairs={{0,2},{1,3},{4,6},{5,7},{16,18},{17,19},{20,22},{21,23},{8,10},{9,... | collective-permute-start | bytes 786440 | tf_op jit(solution)/shard_map/ppermute | solution.py:334
  23.7 3.6 %collective-permute-done.3 = f32[256,256]{1,0:T(8,128)S(1)} collective-permute-done((f32[256,256]{1,0:T(8,128)S(1)}, f32[256,256]{1,0:T(8,128)S(1)}, u32[]{:S(2)}, u32[]{:S(2)}) %collective-permute-start.3) | collective-permute-done | bytes 262176 | tf_op jit(solution)/shard_map/ppermute | solution.py:334
  27.3 1.6 %collective-permute-start.4 = (f32[256,256]{1,0:T(8,128)S(1)}, f32[256,256]{1,0:T(8,128)S(1)}, u32[]{:S(2)}, u32[]{:S(2)}) collective-permute-start(f32[256,256]{1,0:T(8,128)S(1)} %broadcast_select_fusion.3.own), channel_id=1, source_target_pairs={{0,1},{1,0},{2,3},{3,2},{4,5},{5,4},{6,7},{7,6},{8,9},{9,8},{10,11... | collective-permute-start | bytes 786440 | tf_op jit(solution)/shard_map/ppermute | solution.py:381
  28.9 0.0 collective-permute-start.5
  28.9 4.8 %collective-permute-done.4.other = f32[256,256]{1,0:T(8,128)S(1)} collective-permute-done((f32[256,256]{1,0:T(8,128)S(1)}, f32[256,256]{1,0:T(8,128)S(1)}, u32[]{:S(2)}, u32[]{:S(2)}) %collective-permute-start.4) | collective-permute-done | bytes 262176 | tf_op jit(solution)/shard_map/ppermute | solution.py:381
  33.8 0.0 collective-permute-start.6
  33.8 0.0 collective-permute-done.5.own_swapped
  33.8 1.5 %collective-permute-done.6.other_swapped = f32[256,256]{1,0:T(8,128)S(1)} collective-permute-done((f32[256,256]{1,0:T(8,128)S(1)}, f32[256,256]{1,0:T(8,128)S(1)}, u32[]{:S(2)}, u32[]{:S(2)}) %collective-permute-start.6) | collective-permute-done | bytes 262176 | tf_op jit(solution)/shard_map/ppermute | solution.py:383
  35.3 18.6 %update.1 = (f32[256,512]{1,0:T(8,128)}, f32[256,256]{1,0:T(8,128)}, f32[32,512]{1,0:T(8,128)S(1)}) custom-call(s32[3]{0:T(128)S(1)} %pad_add_fusion.flags, f32[256,512]{1,0:T(8,128)S(1)} %bitcast.10, f32[256,256]{1,0:T(8,128)S(1)} %bitcast.12, f32[256,256]{1,0:T(8,128)S(1)} %broadcast_select_fusion.3.own, f32[256,256]{1,0:T(8,128)S(1)} %collective-permute-done.4.other, ...), custom_call_target="tpu_custom_call" | custom-call | flops 10000000000 | bytes 2097152 | tf_op jit(solution)/shard_map/update/pallas_call | solution.py:384
  53.9 0.1 copy.5
  54.0 15.3 %all_to_all.9 = f32[32,1,512]{2,1,0:T(1,128)S(1)} all-to-all(f32[32,1,512]{2,1,0:T(1,128)S(1)} %copy.5), channel_id=1, replica_groups=mesh['row'=4,'col'=8] {'row','col'}, dimensions={0} | all-to-all | bytes 131072 | tf_op jit(solution)/shard_map/all_to_all | solution.py:398
  69.3 0.1 reduce_sum.9
  69.3 0.6 add_sqrt_fusion
  (8 shorter events, 0.1 us)
Async XLA Ops:
  0.7 1.0 %copy-start = (f32[1,256,512]{2,1,0:T(8,128)S(1)}, f32[1,256,512]{2,1,0:T(8,128)}, u32[]{:S(2)}) copy-start(f32[1,256,512]{2,1,0:T(8,128)} %param.2) | copy-start | bytes 1572868
  1.8 2.3 %copy-start.2 = (f32[1,256,256]{2,1,0:T(8,128)S(1)}, f32[1,256,256]{2,1,0:T(8,128)}, u32[]{:S(2)}) copy-start(f32[1,256,256]{2,1,0:T(8,128)} %param.3) | copy-start | bytes 786436
  5.8 3.5 %collective-permute-start = (f32[256,256]{1,0:T(8,128)S(1)}, f32[256,256]{1,0:T(8,128)S(1)}, u32[]{:S(2)}, u32[]{:S(2)}) collective-permute-start(f32[256,256]{1,0:T(8,128)S(1)} %get-tuple-element.8), channel_id=1, source_target_pairs={{0,8},{1,9}} | collective-permute-start | bytes 786440 | tf_op jit(solution)/shard_map/ppermute | solution.py:325
  9.4 7.3 %collective-permute-start.1 = (f32[256,256]{1,0:T(8,128)S(1)}, f32[256,256]{1,0:T(8,128)S(1)}, u32[]{:S(2)}, u32[]{:S(2)}) collective-permute-start(f32[256,256]{1,0:T(8,128)S(1)} %broadcast_select_fusion), channel_id=1, source_target_pairs={{0,4},{1,5},{8,24},{9,25}} | collective-permute-start | bytes 786440 | tf_op jit(solution)/shard_map/ppermute | solution.py:334
  16.8 5.2 %collective-permute-start.2 = (f32[256,256]{1,0:T(8,128)S(1)}, f32[256,256]{1,0:T(8,128)S(1)}, u32[]{:S(2)}, u32[]{:S(2)}) collective-permute-start(f32[256,256]{1,0:T(8,128)S(1)} %broadcast_select_fusion.1), channel_id=1, source_target_pairs={{0,16},{1,17},{4,20},{5,21},{8,12},{9,13},{24,28},{25,29}} | collective-permute-start | bytes 786440 | tf_op jit(solution)/shard_map/ppermute | solution.py:334
  22.0 13.3 %copy-start.1 = (f32[1,256,512]{2,1,0:T(8,128)S(1)}, f32[1,256,512]{2,1,0:T(8,128)}, u32[]{:S(2)}) copy-start(f32[1,256,512]{2,1,0:T(8,128)} %param.2) | copy-start | bytes 1572868
  22.0 5.3 %collective-permute-start.3 = (f32[256,256]{1,0:T(8,128)S(1)}, f32[256,256]{1,0:T(8,128)S(1)}, u32[]{:S(2)}, u32[]{:S(2)}) collective-permute-start(f32[256,256]{1,0:T(8,128)S(1)} %broadcast_select_fusion.2), channel_id=1, source_target_pairs={{0,2},{1,3},{4,6},{5,7},{16,18},{17,19},{20,22},{21,23},{8,10},{9,... | collective-permute-start | bytes 786440 | tf_op jit(solution)/shard_map/ppermute | solution.py:334
  27.3 6.4 %collective-permute-start.4 = (f32[256,256]{1,0:T(8,128)S(1)}, f32[256,256]{1,0:T(8,128)S(1)}, u32[]{:S(2)}, u32[]{:S(2)}) collective-permute-start(f32[256,256]{1,0:T(8,128)S(1)} %broadcast_select_fusion.3.own), channel_id=1, source_target_pairs={{0,1},{1,0},{2,3},{3,2},{4,5},{5,4},{6,7},{7,6},{8,9},{9,8},{10,11... | collective-permute-start | bytes 786440 | tf_op jit(solution)/shard_map/ppermute | solution.py:381
  28.9 4.9 %collective-permute-start.5 = (f32[256,256]{1,0:T(8,128)S(1)}, f32[256,256]{1,0:T(8,128)S(1)}, u32[]{:S(2)}, u32[]{:S(2)}) collective-permute-start(f32[256,256]{1,0:T(8,128)S(1)} %broadcast_select_fusion.3.own), channel_id=1, source_target_pairs={{0,8},{1,9},{2,10},{3,11},{4,12},{5,13},{6,14},{7,15},{8,0},{9,1},... | collective-permute-start | bytes 786440 | tf_op jit(solution)/shard_map/ppermute | solution.py:382
  33.8 1.5 %collective-permute-start.6 = (f32[256,256]{1,0:T(8,128)S(1)}, f32[256,256]{1,0:T(8,128)S(1)}, u32[]{:S(2)}, u32[]{:S(2)}) collective-permute-start(f32[256,256]{1,0:T(8,128)S(1)} %collective-permute-done.4.other), channel_id=1, source_target_pairs={{0,8},{1,9},{2,10},{3,11},{4,12},{5,13},{6,14},{7,15},{8,0},{9,1},... | collective-permute-start | bytes 786440 | tf_op jit(solution)/shard_map/ppermute | solution.py:383
